TPU v7x, 32 devices: a whole 2x2x4 slice. The times are simulated.
32 devices in a mesh: ctx: 8 (over z, y), dp: 4 (over x, core).
Axes of the slice: x: 2, y: 2, z: 4, core: 2. Of those that a mesh axis runs over, the one named last changes fastest.
Arguments:
- grad_out: bfloat16 [4, 3072, 4096], P('dp', 'ctx'), may hold values from -6 to 6
- hidden: bfloat16 [4, 3072, 1792], P('dp', 'ctx'), may hold values from -6 to 6
- down_weight: bfloat16 [1792, 4096], replicated, may hold values from -0.09375 to 0.09375
Outputs:
- grad_hidden: bfloat16 [4, 3072, 1792], P('dp', 'ctx')
- weight_grad: float32 [1792, 4096], P('ctx', 'dp')
- hidden_amax: float32 [4, 1792], P('dp', 'ctx')
- grad_amax: float32 [4, 4096], P('dp', 'ctx')
All inputs are finite; a program needn't handle non-finite values.
Results may differ from a plain program's by a relative error of at most 0.006.
Values may be sent and summed in bfloat16 or wider, within the bound.
No kernel may reach another device: no remote copies, remote signals or barrier semaphores. Data moves between devices by JAX's collectives and lax.ppermute only.
A program may use at most 192 MiB of HBM per device.

v0:
```python
import jax
import jax.numpy as jnp
from jax import lax
from jax.sharding import PartitionSpec as P

ceiling = 448.0


def to_grid(values, peaks):
    scaled = values.astype(jnp.float32) * (ceiling / peaks)[None, :]
    magnitude = jnp.abs(scaled)
    spacing = jnp.full_like(magnitude, 2.0 ** (-9))
    for exponent in range(-5, 9):
        spacing = jnp.where(magnitude >= 2.0**exponent, 2.0 ** (exponent - 3), spacing)
    snapped = jnp.floor(magnitude / spacing + 0.5) * spacing
    return jnp.where(scaled < 0, -snapped, snapped).astype(jnp.bfloat16)


def local_peaks(values):
    return jnp.max(jnp.abs(values.astype(jnp.float32)), axis=0)


def on_device(grad_out, hidden, down_weight):
    gdata = grad_out[0]
    hdata = hidden[0]
    ctx_count = lax.axis_size("ctx")
    position = lax.axis_index("ctx")
    ff_rows = hdata.shape[1] // ctx_count
    width_cols = gdata.shape[1] // ctx_count
    seq_total = gdata.shape[0] * ctx_count * lax.axis_size("dp")
    hpeak, gpeak = lax.pmax((local_peaks(hdata), local_peaks(gdata)), "ctx")
    hpeak, gpeak = (jnp.maximum(hpeak, 1.0), jnp.maximum(gpeak, 1.0))
    result = lax.dot_general(
        gdata, down_weight, (((1,), (1,)), ((), ())), preferred_element_type=jnp.float32
    )
    grad_hidden = result.astype(jnp.bfloat16)[None]
    hquant = to_grid(hdata, hpeak)
    gquant = to_grid(gdata, gpeak)
    hscale = hpeak / ceiling
    gscale = gpeak / ceiling
    product = lax.dot_general(
        hquant, gquant, (((0,), (0,)), ((), ())), preferred_element_type=jnp.float32
    )
    partial_value = lax.psum_scatter(
        product * hscale[:, None] * gscale[None, :], "ctx", scatter_dimension=0, tiled=True
    )
    hidden_amax = lax.dynamic_slice_in_dim(hpeak, position * ff_rows, ff_rows, 0)
    summed = lax.psum_scatter(partial_value, "dp", scatter_dimension=1, tiled=True)
    weight_grad = summed / jnp.sqrt(jnp.float32(seq_total))
    grad_amax = lax.dynamic_slice_in_dim(gpeak, position * width_cols, width_cols, 0)
    return (grad_hidden, weight_grad, hidden_amax[None], grad_amax[None])


def solution(mesh):
    placed = (P("dp", "ctx", None), P("dp", "ctx", None), P())
    return jax.shard_map(
        on_device,
        mesh=mesh,
        in_specs=placed,
        out_specs=(P("dp", "ctx", None), P("ctx", "dp"), P("dp", "ctx"), P("dp", "ctx")),
        check_vma=False,
    )
```

profile of v0, /device:TPU:0, one launch (start us, length us, event | category | flops | bytes accessed | tf_op | source)
XLA Modules:
  0.0 590.8 jit_solution(7346190670684098272)
XLA Ops:
  7.2 0.0 copy-start
  7.2 0.0 reduce-scatter.3.cloned.1.call-start
  7.2 2.4 abs_reduce_fusion
  9.6 1.5 fusion.64
  11.1 38.9 %all-reduce = (f32[4096]{0:T(1024)S(1)}, f32[1792]{0:T(1024)S(1)}) all-reduce(f32[4096]{0:T(1024)S(1)} %abs_reduce_fusion, f32[1792]{0:T(1024)S(1)} %fusion.64), channel_id=1, replica_groups=mesh['ctx'=8,'dp'=4] {'ctx'}, use_global_device_ids=true, to_apply=%region_3.0 | all-reduce | flops 5888 | bytes 47104 | tf_op jit(solution)/shard_map/pmax | solution.py:31
  50.0 0.0 copy-done
  50.0 28.1 %multiply_multiply_fusion = f32[1792,4096]{1,0:T(8,128)} fusion(f32[4096]{0:T(1024)S(1)} %get-tuple-element.8, f32[1792]{0:T(1024)S(1)} %get-tuple-element.11, bf16[1,384,4096]{2,1,0:T(8,128)(2,1)S(1)} %copy-done, f32[4096]{0:T(1024)S(1)} %get-tuple-element.7, bf16[1,384,1792]{2,1,0:T(8,128)(2,1)} %param.4, f32[1792]{0:T(1024)S(1)} %get-tuple-element.10), kind=kOutput, calls=%fused_computation | convolution fusion | flops 5740003328 | bytes 33929216 | tf_op jit(solution)/shard_map/dot_general | solution.py:41
  78.1 0.0 reduce-scatter.3.cloned.1.call-update
  78.1 0.0 reduce-scatter.5.cloned.1.call-start
  78.2 460.8 %reduce-scatter.3.cloned.1.call-done = f32[224,4096]{1,0:T(8,128)} async-done(((f32[1792,4096]{1,0:T(8,128)}), f32[224,4096]{1,0:T(8,128)}) %reduce-scatter.3.cloned.1.call-update) | async-done | bytes 3670032 | tf_op jit(solution)/shard_map/reduce_scatter | solution.py:44
  539.0 0.0 reduce-scatter.5.cloned.1.call-update
  539.0 0.7 dynamic_slice.7
  539.7 0.6 dynamic_slice.6
  540.3 10.4 %fusion.66 = bf16[1,384,1792]{2,1,0:T(8,128)(2,1)} fusion(bf16[1792,4096]{1,0:T(8,128)(2,1)} %param.5, bf16[1,384,4096]{2,1,0:T(8,128)(2,1)S(1)} %copy-done), kind=kOutput, calls=%fused_computation.70 | convolution fusion | flops 5637832704 | bytes 19202048 | tf_op jit(solution)/shard_map/dot_general | solution.py:33
  550.7 31.0 %reduce-scatter.5.cloned.1.call-done = f32[224,1024]{1,0:T(8,128)} async-done(((f32[224,4096]{1,0:T(8,128)}), f32[224,1024]{1,0:T(8,128)}) %reduce-scatter.5.cloned.1.call-update) | async-done | bytes 917520 | tf_op jit(solution)/shard_map/reduce_scatter | solution.py:48
  581.8 2.2 broadcast_multiply_fusion
  (2 shorter events, 0.0 us)
Async XLA Ops:
  7.2 42.9 %copy-start = (bf16[1,384,4096]{2,1,0:T(8,128)(2,1)S(1)}, bf16[1,384,4096]{2,1,0:T(8,128)(2,1)}, u32[]{:S(2)}) copy-start(bf16[1,384,4096]{2,1,0:T(8,128)(2,1)} %param.3) | copy-start | bytes 9437188
  7.2 531.8 %reduce-scatter.3.cloned.1.call-start = ((), (), s32[]{:S(2)}) async-start(), calls=%async_computation.2 | async-start | bytes 33030144 | tf_op jit(solution)/shard_map/reduce_scatter | solution.py:44
  78.1 503.6 %reduce-scatter.5.cloned.1.call-start = ((), (), s32[]{:S(2)}) async-start(), calls=%async_computation.3 | async-start | bytes 4587520 | tf_op jit(solution)/shard_map/reduce_scatter | solution.py:48
Sparse Core Ops, SparseCore 0:
  78.2 460.7 reduce-scatter.2
  541.5 40.1 reduce-scatter.4
where the time goes:
time: 591 us
  waiting for transfers between devices  492 us (83%)
  blocking collectives  38.9 us (7%)
  matrix products  38.5 us (7%)
  between operations  14.1 us (2%)
  other arithmetic  6.13 us (1%)
    reduce_scatter x1, waiting for transfers between devices, on_device(): lax.psum_scatter(product * hscale[:, None] * gscale[None, :], 'ctx', scat...  461 us
    pmax x1, blocking collectives, on_device(): hpeak, gpeak = lax.pmax((local_peaks(hdata), local_peaks(gdata)), 'ctx')  38.9 us
    reduce_scatter x1, waiting for transfers between devices, on_device(): lax.psum_scatter(partial_value, 'dp', scatter_dimension=1, tiled=True)  31 us
    dot_general x1, matrix products, on_device(): lax.dot_general(hquant, gquant, (((0,), (0,)), ((), ())), preferred_eleme...  28.1 us
  transfers between devices with their start and end apart: 2, of which 2 were waited for; matrix products, arithmetic and copies ran while one was open for 2% of the time, Pallas kernels for 0%

commit v1 on v0

v1 whole, which is shorter than its diff:
```python
import jax
import jax.numpy as jnp
from jax import lax
from jax.experimental import pallas as pl
from jax.experimental.pallas import tpu as pltpu
from jax.sharding import PartitionSpec as P


ceiling = 448.0
LANES = 128


def to_grid(values, factor, scale):
    scaled = values.astype(jnp.float32) * factor
    magnitude = jnp.abs(scaled)
    wide = magnitude * (2.0**23 + 1.0)
    base = jnp.maximum(wide - wide * (1.0 - 2.0**-24), 2.0**-6)
    magic = base * (1.5 * 2.0**20)
    near = (scaled + magic) - magic
    short = magnitude - jnp.abs(near)
    tie = short >= base * (0.0625 * (1.0 - 2.0**-24))
    near = jnp.where(tie, scaled + (scaled - near), near)
    return (near * scale).astype(jnp.bfloat16)


def row_order(count):
    order, bit = [0], count
    while bit > 1:
        bit //= 2
        order = [k ^ bit for k in order] + order
    return order


def turn_rows(hdata, blocks, ctx_count):
    tokens, ff = hdata.shape
    rows = ff // ctx_count
    wide = ff // 2 if (ff // 2) % LANES == 0 else LANES
    steps = ff // wide

    def body(order, source, sent, kept, peaks, turned):
        step = pl.program_id(0)
        tile = source[...]
        peaks[...] = jnp.max(jnp.abs(tile.astype(jnp.float32)), axis=0, keepdims=True)
        turned[pl.ds(pl.multiple_of(step * wide, wide), wide), :] = tile.T

        @pl.when(step == steps - 1)
        def _():
            for half, target in enumerate((sent, kept)):
                for j in range(ctx_count // 2):
                    block = order[half * (ctx_count // 2) + j]
                    start = pl.multiple_of(block * rows, 16)
                    target[j * rows : (j + 1) * rows, :] = turned[pl.ds(start, rows), :]

    half_shape = jax.ShapeDtypeStruct((ff // 2, tokens), jnp.bfloat16)
    return pl.pallas_call(
        body,
        out_shape=(half_shape, half_shape, jax.ShapeDtypeStruct((1, ff), jnp.float32)),
        grid_spec=pltpu.PrefetchScalarGridSpec(
            num_scalar_prefetch=1,
            grid=(steps,),
            in_specs=[pl.BlockSpec((tokens, wide), lambda i, o: (0, i))],
            out_specs=[
                pl.BlockSpec((ff // 2, tokens), lambda i, o: (0, 0)),
                pl.BlockSpec((ff // 2, tokens), lambda i, o: (0, 0)),
                pl.BlockSpec((1, wide), lambda i, o: (0, i)),
            ],
            scratch_shapes=[pltpu.VMEM((ff, tokens), jnp.bfloat16)],
        ),
        name="turn_rows",
    )(blocks, hdata)


def divide(peak):
    quotient = ceiling / peak
    wide = quotient * 4097.0
    high = wide - (wide - quotient)
    rest = (ceiling - high * peak) - (quotient - high) * peak
    return quotient + rest * (quotient * (1.0 / ceiling))


def scale_tables(peaks, where_to, ff, own_cols, ctx_count):
    count = len(peaks)
    rows = ff // ctx_count

    def body(where_ref, *refs):
        sources, (cols, gtable), (by_lane, by_row) = refs[:count], refs[count : count + 2], refs[count + 2 :]
        start = pl.multiple_of(ff + where_ref[ctx_count] * own_cols, LANES)
        for r in range(count):
            peak = sources[r][:, :ff]
            by_lane[r : r + 1, :] = divide(peak)
            by_lane[count + r : count + r + 1, :] = peak / ceiling
            peak = sources[r][:, pl.ds(start, own_cols)]
            gtable[r : r + 1, :] = divide(peak)
            gtable[count + r : count + r + 1, :] = peak / ceiling
        for c in range(0, ff, LANES):
            by_row[c : c + LANES, :] = by_lane[:, c : c + LANES].T
        for j in range(ctx_count):
            begin = pl.multiple_of(where_ref[j] * rows, 8)
            cols[j * rows : (j + 1) * rows, :] = by_row[pl.ds(begin, rows), :]

    whole = lambda i, w: (0, 0)
    return pl.pallas_call(
        body,
        out_shape=(
            jax.ShapeDtypeStruct((ff, 2 * count), jnp.float32),
            jax.ShapeDtypeStruct((2 * count, own_cols), jnp.float32),
        ),
        grid_spec=pltpu.PrefetchScalarGridSpec(
            num_scalar_prefetch=1,
            grid=(1,),
            in_specs=[pl.BlockSpec(peaks[0].shape, whole)] * count,
            out_specs=[pl.BlockSpec((ff, 2 * count), whole), pl.BlockSpec((2 * count, own_cols), whole)],
            scratch_shapes=[pltpu.VMEM((2 * count, ff), jnp.float32), pltpu.VMEM((ff, 2 * count), jnp.float32)],
        ),
        name="scale_tables",
    )(where_to, *peaks)


def quantize_rows(sources, cols, offset, tile):
    rows, tokens = sources[0].shape
    count = len(sources)

    def body(*refs):
        cols_ref, out = refs[count], refs[count + 1]
        for r in range(count):
            out[:, r * tokens : (r + 1) * tokens] = to_grid(
                refs[r][...], cols_ref[:, r : r + 1], cols_ref[:, count + r : count + r + 1]
            )

    return pl.pallas_call(
        body,
        out_shape=jax.ShapeDtypeStruct((rows, count * tokens), jnp.bfloat16),
        grid=(rows // tile,),
        in_specs=[pl.BlockSpec((tile, tokens), lambda i: (i, 0))] * count
        + [pl.BlockSpec((tile, 2 * count), lambda i: (i + offset // tile, 0))],
        out_specs=pl.BlockSpec((tile, count * tokens), lambda i: (i, 0)),
        cost_estimate=pl.CostEstimate(
            flops=2000 * rows * tokens * count, transcendentals=0, bytes_accessed=4 * rows * tokens * count
        ),
        name="quantize_rows",
    )(*sources, cols)


def product(left, right):
    return lax.dot_general(left, right, (((1,), (0,)), ((), ())), preferred_element_type=jnp.float32)


def quantize_and_multiply(hq, sources, gtable, start, tile):
    rows, depth = hq.shape
    tokens, width = sources[2].shape
    count = len(sources)

    def body(*refs):
        hq_ref, table = refs[:2]
        raw = refs[2 : 2 + count]
        out, gq = refs[2 + count :]

        @pl.when(pl.program_id(0) == 0)
        def _():
            for r in range(count):
                gq[r * tokens : (r + 1) * tokens, :] = to_grid(
                    raw[r][:, start : start + width] if r < 2 else raw[r][...],
                    table[r : r + 1, start : start + width],
                    table[count + r : count + r + 1, start : start + width],
                )

        out[...] = product(hq_ref[...], gq[...]).astype(jnp.bfloat16)

    whole = lambda i: (0, 0)
    return pl.pallas_call(
        body,
        out_shape=(
            jax.ShapeDtypeStruct((rows, width), jnp.bfloat16),
            jax.ShapeDtypeStruct((depth, width), jnp.bfloat16),
        ),
        grid=(rows // tile,),
        in_specs=[pl.BlockSpec((tile, depth), lambda i: (i, 0)), pl.BlockSpec(gtable.shape, whole)]
        + [pl.BlockSpec(source.shape, whole) for source in sources],
        out_specs=[pl.BlockSpec((tile, width), lambda i: (i, 0)), pl.BlockSpec((depth, width), whole)],
        cost_estimate=pl.CostEstimate(
            flops=4 * rows * depth * width, transcendentals=0, bytes_accessed=2 * depth * (rows + width)
        ),
        name="quantize_and_multiply",
    )(hq, gtable, *sources)


def finish(rows_in, cols, gq, arrived, tile):
    raw = isinstance(rows_in, list)
    inputs = rows_in if raw else [rows_in]
    count = len(inputs)
    rows, tokens = inputs[0].shape
    depth, width = gq.shape
    steps = rows // tile
    cut = steps // 2

    def body(*refs):
        gq_ref, arrived_ref = refs[:2]
        sources, rest = refs[2 : 2 + count], refs[2 + count :]
        step = pl.program_id(0)
        if raw:
            cols_ref, send, keep, hq = rest
            for r in range(count):
                hq[:, r * tokens : (r + 1) * tokens] = to_grid(
                    sources[r][...], cols_ref[:, r : r + 1], cols_ref[:, count + r : count + r + 1]
                )
        else:
            send, keep = rest
            hq = sources[0]
        total = product(hq[...], gq_ref[...]) + arrived_ref[...].astype(jnp.float32)

        @pl.when(step < cut)
        def _():
            send[...] = total.astype(jnp.bfloat16)

        @pl.when(step >= cut)
        def _():
            keep[...] = total

    by_step = lambda i: (i, 0)
    in_specs = [pl.BlockSpec((depth, width), lambda i: (0, 0)), pl.BlockSpec((tile, width), by_step)]
    in_specs += [pl.BlockSpec((tile, tokens), by_step)] * count
    operands = [gq, arrived] + inputs
    out_shape = [
        jax.ShapeDtypeStruct((cut * tile, width), jnp.bfloat16),
        jax.ShapeDtypeStruct((cut * tile, width), jnp.float32),
    ]
    out_specs = [
        pl.BlockSpec((tile, width), lambda i: (jnp.minimum(i, cut - 1), 0)),
        pl.BlockSpec((tile, width), lambda i: (jnp.maximum(i - cut, 0), 0)),
    ]
    if raw:
        in_specs.append(pl.BlockSpec((tile, 2 * count), lambda i: (i + steps, 0)))
        operands.append(cols)
        out_shape.append(jax.ShapeDtypeStruct((rows, depth), jnp.bfloat16))
        out_specs.append(pl.BlockSpec((tile, depth), by_step))
    return pl.pallas_call(
        body,
        out_shape=out_shape,
        grid=(steps,),
        in_specs=in_specs,
        out_specs=out_specs,
        cost_estimate=pl.CostEstimate(
            flops=4 * rows * depth * width, transcendentals=0, bytes_accessed=2 * depth * (rows + width)
        ),
        name="finish",
    )(*operands)


def split_width(width, parts):
    units = width // LANES
    parts = min(parts, units)
    sizes = [units // parts + (1 if i < units % parts else 0) for i in range(parts)]
    return [size * LANES for size in sizes]


def on_device(grad_out, hidden, down_weight):
    gdata = grad_out[0]
    hdata = hidden[0]
    tokens = gdata.shape[0]
    ctx_count, dp_count = lax.axis_size("ctx"), lax.axis_size("dp")
    position, place = lax.axis_index("ctx"), lax.axis_index("dp")
    ff, width = hdata.shape[1], gdata.shape[1]
    ff_rows, width_cols = ff // ctx_count, width // ctx_count
    own_cols = width // dp_count
    seq_total = tokens * ctx_count * dp_count
    tile = 2 * ff_rows

    def swap(value, axis, distance):
        count = ctx_count if axis == "ctx" else dp_count
        return lax.ppermute(value, axis, [(i, i ^ distance) for i in range(count)])

    sizes = split_width(own_cols, 3)
    starts = [sum(sizes[:j]) for j in range(len(sizes))]

    def column_block(k, start, size):
        return lax.dynamic_slice(gdata, (0, (place ^ k) * own_cols + start), (tokens, size))

    own_block = column_block(0, 0, own_cols)
    near_block = swap(column_block(1, 0, own_cols), "dp", 1)
    chunks = []
    for start, size in zip(starts, sizes):
        parts = [own_block, near_block]
        for k in range(2, dp_count):
            parts.append(swap(column_block(k, start, size), "dp", k))
        chunks.append(parts)

    blocks = position ^ jnp.array(row_order(ctx_count), jnp.int32)
    sent_rows, kept_rows, hpeak = turn_rows(hdata, blocks, ctx_count)

    def spread(value):
        slots = [value, swap(value, "dp", 1)]
        for k in range(2, dp_count, 2):
            far = swap(value, "dp", k)
            slots += [far, swap(far, "dp", 1)]
        return slots

    sent_slots = spread(sent_rows)
    kept_slots = spread(kept_rows)

    gpeak = jnp.max(jnp.abs(gdata.astype(jnp.float32)), axis=0, keepdims=True)
    peaks = jnp.concatenate([hpeak, gpeak], axis=1)
    bit = 1
    while bit < ctx_count:
        peaks = jnp.maximum(peaks, swap(peaks, "ctx", bit))
        bit *= 2
    peaks = jnp.maximum(peaks, 1.0)
    hidden_amax = lax.dynamic_slice(peaks, (0, position * ff_rows), (1, ff_rows))
    grad_amax = lax.dynamic_slice(peaks, (0, ff + position * width_cols), (1, width_cols))
    all_peaks = [peaks] + [swap(peaks, "dp", k) for k in range(1, dp_count)]
    where_to = jnp.concatenate([blocks, place[None]])
    cols, gtable = scale_tables(all_peaks, where_to, ff, own_cols, ctx_count)
    hq_sent = quantize_rows(sent_slots, cols, 0, ff_rows)
    rows_in, results = kept_slots, []
    for j, (start, size) in enumerate(zip(starts, sizes)):
        outgoing, gq = quantize_and_multiply(hq_sent, chunks[j], gtable, start, tile)
        arrived = swap(outgoing, "ctx", 1)
        send, keep, *quantized = finish(rows_in, cols, gq, arrived, ff_rows)
        rows_in = quantized[0] if quantized else rows_in
        bit = 2
        while True:
            arrived = swap(send, "ctx", bit)
            total = keep + arrived.astype(jnp.float32)
            bit *= 2
            if bit == ctx_count:
                break
            cut = total.shape[0] // 2
            send, keep = total[:cut].astype(jnp.bfloat16), total[cut:]
        results.append(total)
    weight_grad = jnp.concatenate(results, axis=1) / jnp.sqrt(jnp.float32(seq_total))

    result = lax.dot_general(
        gdata, down_weight, (((1,), (1,)), ((), ())), preferred_element_type=jnp.float32
    )
    grad_hidden = result.astype(jnp.bfloat16)[None]
    return (grad_hidden, weight_grad, hidden_amax, grad_amax)


def solution(mesh):
    placed = (P("dp", "ctx", None), P("dp", "ctx", None), P())

    return jax.shard_map(
        on_device,
        mesh=mesh,
        in_specs=placed,
        out_specs=(P("dp", "ctx", None), P("ctx", "dp"), P("dp", "ctx"), P("dp", "ctx")),
        check_vma=False,
    )
```

time: 591 us -> 164 us (0.28)
  waiting for transfers between devices: 492 us -> 61.4 us
  Pallas kernels: 0 us -> 48 us
  blocking collectives: 38.9 us -> 0 us
  starting transfers between devices: 0.08 us -> 30.4 us
  matrix products: 38.5 us -> 10.4 us
  between operations: 14.1 us -> 0.8 us
    reduce_scatter x2 -> x0, waiting for transfers between devices: 492 us -> none  [the longest x1 461 us: on_device(): lax.psum_scatter(product * hscale[:, None] * gscale[None, :], 'ctx', scat...]
    ppermute x0 -> x28, waiting for transfers between devices: none -> 61.4 us  [swap(): return lax.ppermute(value, axis, [(i, i ^ distance) for i in range(count)])]
    pallas_call x0 -> x9, Pallas kernels: none -> 48 us  [the longest x3 18.9 us: finish(): pl.pallas_call(body, out_shape=out_shape, grid=(steps,), in_specs=in_spec...]
    pmax x1 -> x0, blocking collectives: 38.9 us -> none  [on_device(): hpeak, gpeak = lax.pmax((local_peaks(hdata), local_peaks(gdata)), 'ctx')]
    ppermute x0 -> x28, starting transfers between devices: none -> 30.4 us  [swap(): return lax.ppermute(value, axis, [(i, i ^ distance) for i in range(count)])]
    dot_general x1 -> x0, matrix products: 28.1 us -> none  [on_device(): lax.dot_general(hquant, gquant, (((0,), (0,)), ((), ())), preferred_eleme...]
  transfers between devices with their start and end apart: 2 -> 28, of which waited for: 2 -> 13; matrix products, arithmetic and copies ran while one was open for 2% -> 11% of each run, Pallas kernels for 0% -> 27%
where the time goes in v1:
time: 164 us; the launch traced here: 163 us
  waiting for transfers between devices  61.4 us (37%)
  Pallas kernels  48 us (29%)
  starting transfers between devices  30.4 us (19%)
  matrix products  10.4 us (6%)
  other arithmetic  6.28 us (4%)
  local copies, waits for them, and re-layouts  5.67 us (3%)
    ppermute x28, waiting for transfers between devices, swap(): return lax.ppermute(value, axis, [(i, i ^ distance) for i in range(count)])  61.4 us
    ppermute x28, starting transfers between devices, swap(): return lax.ppermute(value, axis, [(i, i ^ distance) for i in range(count)])  30.4 us
    pallas_call x3, Pallas kernels, finish(): pl.pallas_call(body, out_shape=out_shape, grid=(steps,), in_specs=in_spec...  18.9 us
    pallas_call x3, Pallas kernels, quantize_and_multiply(): pl.pallas_call(body, out_shape=(jax.ShapeDtypeStruct((rows, width), jnp.b...  16.4 us
    dot_general x1, matrix products, on_device(): lax.dot_general(gdata, down_weight, (((1,), (1,)), ((), ())), preferred_e...  10.4 us
    pallas_call x1, Pallas kernels, quantize_rows(): pl.pallas_call(body, out_shape=jax.ShapeDtypeStruct((rows, count * tokens...  6.39 us
    pallas_call x1, Pallas kernels, turn_rows(): pl.pallas_call(body, out_shape=(half_shape, half_shape, jax.ShapeDtypeStr...  3.55 us
  transfers between devices with their start and end apart: 28, of which 13 were waited for; matrix products, arithmetic and copies ran while one was open for 11% of the time, Pallas kernels for 27%

profile of v1, /device:TPU:0, one launch (start us, length us, event | category | flops | bytes accessed | tf_op | source)
XLA Modules:
  0.0 163.0 jit_solution(12124115341867902532)
XLA Ops:
  0.6 0.0 copy-start.10
  0.7 2.4 %abs_reduce_fusion = f32[4096]{0:T(1024)S(1)} fusion(bf16[1,384,4096]{2,1,0:T(8,128)(2,1)} %param.4), kind=kLoop, calls=%fused_computation | loop fusion | flops 4714496 | bytes 3162112 | tf_op jit(solution)/shard_map/reduce_max | solution.py:300
  3.1 0.5 broadcast_xor_fusion.order
  3.6 3.6 %turn_rows.1 = (bf16[896,384]{1,0:T(8,128)(2,1)}, bf16[896,384]{1,0:T(8,128)(2,1)}, f32[1,1792]{1,0:T(1,128)}) custom-call(s32[8]{0:T(128)} %broadcast_xor_fusion.order, bf16[384,1792]{1,0:T(8,128)(2,1)} %bitcast.30), custom_call_target="tpu_custom_call" | custom-call | tf_op jit(solution)/shard_map/turn_rows/pallas_call | solution.py:55
  7.1 0.7 pad_maximum_fusion
  7.8 3.1 %collective-permute-start.3 = (f32[1,5888]{1,0:T(1,128)S(1)}, f32[1,5888]{1,0:T(1,128)S(1)}, u32[]{:S(2)}, u32[]{:S(2)}) collective-permute-start(f32[1,5888]{1,0:T(1,128)S(1)} %pad_maximum_fusion), channel_id=1, source_target_pairs={{0,4},{4,0},{8,12},{12,8},{16,20},{20,16},{24,28},{28,24},{1,5},{5... | collective-permute-start | bytes 70664 | tf_op jit(solution)/shard_map/ppermute | solution.py:270
  10.9 1.5 collective-permute-start.1
  12.4 0.0 collective-permute-start
  12.4 0.3 collective-permute-done.3
  12.7 0.7 fusion.8
  13.4 0.0 copy-start.8
  13.4 2.1 %collective-permute-start.4 = (f32[1,5888]{1,0:T(1,128)S(1)}, f32[1,5888]{1,0:T(1,128)S(1)}, u32[]{:S(2)}, u32[]{:S(2)}) collective-permute-start(f32[1,5888]{1,0:T(1,128)S(1)} %fusion.8), channel_id=1, source_target_pairs={{0,8},{4,12},{8,0},{12,4},{16,24},{20,28},{24,16},{28,20},{1,9},{5... | collective-permute-start | bytes 70664 | tf_op jit(solution)/shard_map/ppermute | solution.py:270
  15.6 1.0 dynamic-slice_bitcast_fusion.2
  16.5 1.5 collective-permute-start.10
  18.1 2.7 %collective-permute-start.5 = (f32[1,5888]{1,0:T(1,128)S(1)}, f32[1,5888]{1,0:T(1,128)S(1)}, u32[]{:S(2)}, u32[]{:S(2)}) collective-permute-start(f32[1,5888]{1,0:T(1,128)S(1)} %max.16), channel_id=1, source_target_pairs={{0,16},{4,20},{8,24},{12,28},{16,0},{20,4},{24,8},{28,12},{1,17},{... | collective-permute-start | bytes 70664 | tf_op jit(solution)/shard_map/ppermute | solution.py:270
  20.7 1.3 dynamic-slice_bitcast_fusion
  22.0 7.5 %collective-permute-done.1.refs_2_ = bf16[896,384]{1,0:T(8,128)(2,1)} collective-permute-done((bf16[896,384]{1,0:T(8,128)(2,1)}, bf16[896,384]{1,0:T(8,128)(2,1)}, u32[]{:S(2)}, u32[]{:S(2)}) %collective-permute-start.1) | collective-permute-done | bytes 688160 | tf_op jit(solution)/shard_map/ppermute | solution.py:270
  29.6 0.6 collective-permute-start.6
  30.2 1.9 %collective-permute-done.6.refs_1_ = f32[1,5888]{1,0:T(1,128)S(1)} collective-permute-done((f32[1,5888]{1,0:T(1,128)S(1)}, f32[1,5888]{1,0:T(1,128)S(1)}, u32[]{:S(2)}, u32[]{:S(2)}) %collective-permute-start.6) | collective-permute-done | bytes 23584 | tf_op jit(solution)/shard_map/ppermute | solution.py:270
  32.0 1.5 collective-permute-start.7
  33.5 2.3 %collective-permute-done.7.refs_2_ = f32[1,5888]{1,0:T(1,128)S(1)} collective-permute-done((f32[1,5888]{1,0:T(1,128)S(1)}, f32[1,5888]{1,0:T(1,128)S(1)}, u32[]{:S(2)}, u32[]{:S(2)}) %collective-permute-start.7) | collective-permute-done | bytes 23584 | tf_op jit(solution)/shard_map/ppermute | solution.py:270
  35.8 0.1 collective-permute-start.8
  35.9 3.4 %collective-permute-done.8.refs_3_ = f32[1,5888]{1,0:T(1,128)S(1)} collective-permute-done((f32[1,5888]{1,0:T(1,128)S(1)}, f32[1,5888]{1,0:T(1,128)S(1)}, u32[]{:S(2)}, u32[]{:S(2)}) %collective-permute-start.8) | collective-permute-done | bytes 23584 | tf_op jit(solution)/shard_map/ppermute | solution.py:270
  39.3 1.3 collective-permute-start.14
  40.6 0.8 dynamic-slice_bitcast_fusion.6
  41.4 0.2 collective-permute-start.11
  41.5 0.6 pad_add_fusion.where_ref
  42.1 2.8 %scale_tables.1 = (f32[1792,8]{1,0:T(8,128)}, f32[8,1024]{1,0:T(8,128)}) custom-call(s32[9]{0:T(128)} %pad_add_fusion.where_ref, f32[1,5888]{1,0:T(1,128)} %copy-done.4, f32[1,5888]{1,0:T(1,128)} %copy-done.5, f32[1,5888]{1,0:T(1,128)} %copy-done.6, f32[1,5888]{1,0:T(1,128)} %copy-done.7), custom_call_target="tpu_custom_call" | custom-call | tf_op jit(solution)/shard_map/scale_tables/pallas_call | solution.py:102
  44.9 0.6 collective-permute-start.18
  45.5 1.5 collective-permute-start.19
  47.0 6.4 %quantize_rows.1.refs_0_ = bf16[896,1536]{1,0:T(8,128)(2,1)} custom-call(bf16[896,384]{1,0:T(8,128)(2,1)} %get-tuple-element.22.refs_0_, bf16[896,384]{1,0:T(8,128)(2,1)} %collective-permute-done.refs_1_, bf16[896,384]{1,0:T(8,128)(2,1)} %collective-permute-done.1.refs_2_, bf16[896,384]{1,0:T(8,128)(2,1)} %collective-permute-done.2.refs_3_, ...), custom_call_target="tpu_custom_call" | custom-call | flops 2752512000 | bytes 5505024 | tf_op jit(solution)/shard_map/quantize_rows/pallas_call | solution.py:130
  53.3 9.7 %collective-permute-done.11.refs_5_ = bf16[384,384]{1,0:T(8,128)(2,1)} collective-permute-done((bf16[384,384]{1,0:T(8,128)(2,1)}, bf16[384,384]{1,0:T(8,128)(2,1)}, u32[]{:S(2)}, u32[]{:S(2)}) %collective-permute-start.11) | collective-permute-done | bytes 294944 | tf_op jit(solution)/shard_map/ppermute | solution.py:270
  63.0 1.0 collective-permute-start.13
  64.1 1.3 collective-permute-start.23
  65.3 5.9 %quantize_and_multiply.3 = (bf16[896,384]{1,0:T(8,128)(2,1)}, bf16[1536,384]{1,0:T(8,128)(2,1)}) custom-call(bf16[896,1536]{1,0:T(8,128)(2,1)} %quantize_rows.1.refs_0_, f32[8,1024]{1,0:T(8,128)} %get-tuple-element.25.refs_1_, bf16[384,1024]{1,0:T(8,128)(2,1)} %get-tuple-element.47.refs_2_, bf16[384,1024]{1,0:T(8,128)(2,1)} %collective-permute-done.9.refs_3_, ...), custom_call_target="tpu_custom_call" | custom-call | flops 2113929216 | bytes 3932160 | tf_op jit(solution)/shard_map/quantize_and_multiply/pallas_call | solution.py:170
  71.2 0.1 collective-permute-start.24
  71.3 0.8 collective-permute-start.15
  72.1 3.5 %collective-permute-done.19.refs_5_ = bf16[384,384]{1,0:T(8,128)(2,1)} collective-permute-done((bf16[384,384]{1,0:T(8,128)(2,1)S(1)}, bf16[384,384]{1,0:T(8,128)(2,1)}, u32[]{:S(2)}, u32[]{:S(2)}) %collective-permute-start.19) | collective-permute-done | bytes 294944 | tf_op jit(solution)/shard_map/ppermute | solution.py:270
  75.6 0.5 collective-permute-start.12
  76.1 5.9 %quantize_and_multiply.4 = (bf16[896,384]{1,0:T(8,128)(2,1)}, bf16[1536,384]{1,0:T(8,128)(2,1)}) custom-call(bf16[896,1536]{1,0:T(8,128)(2,1)} %quantize_rows.1.refs_0_, f32[8,1024]{1,0:T(8,128)} %get-tuple-element.25.refs_1_, bf16[384,1024]{1,0:T(8,128)(2,1)} %get-tuple-element.47.refs_2_, bf16[384,1024]{1,0:T(8,128)(2,1)} %collective-permute-done.9.refs_3_, ...), custom_call_target="tpu_custom_call" | custom-call | flops 2113929216 | bytes 3932160 | tf_op jit(solution)/shard_map/quantize_and_multiply/pallas_call | solution.py:170
  82.0 1.5 collective-permute-start.20
  83.5 0.1 collective-permute-done.24.refs_5_
  83.6 4.6 %quantize_and_multiply.5 = (bf16[896,256]{1,0:T(8,128)(2,1)}, bf16[1536,256]{1,0:T(8,128)(2,1)}) custom-call(bf16[896,1536]{1,0:T(8,128)(2,1)} %quantize_rows.1.refs_0_, f32[8,1024]{1,0:T(8,128)} %get-tuple-element.25.refs_1_, bf16[384,1024]{1,0:T(8,128)(2,1)} %get-tuple-element.47.refs_2_, bf16[384,1024]{1,0:T(8,128)(2,1)} %collective-permute-done.9.refs_3_, ...), custom_call_target="tpu_custom_call" | custom-call | flops 1409286144 | bytes 3538944 | tf_op jit(solution)/shard_map/quantize_and_multiply/pallas_call | solution.py:170
  88.2 0.4 collective-permute-start.25
  88.6 10.4 %fusion.5 = bf16[1,384,1792]{2,1,0:T(8,128)(2,1)} fusion(bf16[1792,4096]{1,0:T(8,128)(2,1)} %param.6, bf16[1,384,4096]{2,1,0:T(8,128)(2,1)S(1)} %copy-done), kind=kOutput, calls=%fused_computation.4 | convolution fusion | flops 5637832704 | bytes 19202048 | tf_op jit(solution)/shard_map/dot_general | solution.py:331
  99.0 1.3 constant_dynamic-slice_fusion
  100.2 8.6 %finish.3 = (bf16[448,384]{1,0:T(8,128)(2,1)}, f32[448,384]{1,0:T(8,128)}, bf16[896,1536]{1,0:T(8,128)(2,1)}) custom-call(bf16[1536,384]{1,0:T(8,128)(2,1)} %get-tuple-element.26.refs_0_, bf16[896,384]{1,0:T(8,128)(2,1)} %collective-permute-done.12.refs_1_, bf16[896,384]{1,0:T(8,128)(2,1)} %get-tuple-element.28.refs_2_, ...), custom_call_target="tpu_custom_call" | custom-call | flops 2113929216 | bytes 3932160 | tf_op jit(solution)/shard_map/finish/pallas_call | solution.py:236
  108.9 9.7 %collective-permute-done.25.refs_1_ = bf16[896,256]{1,0:T(8,128)(2,1)} collective-permute-done((bf16[896,256]{1,0:T(8,128)(2,1)}, bf16[896,256]{1,0:T(8,128)(2,1)}, u32[]{:S(2)}, u32[]{:S(2)}) %collective-permute-start.25) | collective-permute-done | bytes 458784 | tf_op jit(solution)/shard_map/ppermute | solution.py:270
  118.6 4.8 %finish.5 = (bf16[448,256]{1,0:T(8,128)(2,1)}, f32[448,256]{1,0:T(8,128)}) custom-call(bf16[1536,256]{1,0:T(8,128)(2,1)} %get-tuple-element.36.refs_0_, bf16[896,256]{1,0:T(8,128)(2,1)} %collective-permute-done.25.refs_1_, bf16[896,1536]{1,0:T(8,128)(2,1)} %get-tuple-element.33.refs_2_), custom_call_target="tpu_custom_call" | custom-call | flops 1409286144 | bytes 3538944 | tf_op jit(solution)/shard_map/finish/pallas_call | solution.py:236
  123.4 1.6 collective-permute-start.26
  125.0 1.3 constant_dynamic-slice_fusion.1
  126.2 0.5 collective-permute-start.16
  126.7 5.5 %finish.4 = (bf16[448,384]{1,0:T(8,128)(2,1)}, f32[448,384]{1,0:T(8,128)}) custom-call(bf16[1536,384]{1,0:T(8,128)(2,1)} %get-tuple-element.31.refs_0_, bf16[896,384]{1,0:T(8,128)(2,1)} %collective-permute-done.20.refs_1_, bf16[896,1536]{1,0:T(8,128)(2,1)} %get-tuple-element.33.refs_2_), custom_call_target="tpu_custom_call" | custom-call | flops 2113929216 | bytes 3932160 | tf_op jit(solution)/shard_map/finish/pallas_call | solution.py:236
  132.2 1.5 collective-permute-start.21
  133.8 2.7 %collective-permute-start.27 = (bf16[224,256]{1,0:T(8,128)(2,1)S(1)}, bf16[224,256]{1,0:T(8,128)(2,1)S(1)}, u32[]{:S(2)}, u32[]{:S(2)}) collective-permute-start(bf16[224,256]{1,0:T(8,128)(2,1)S(1)} %slice.41), channel_id=1, source_target_pairs={{0,16},{4,20},{8,24},{12,28},{16,0},{20,4},{24,8},{28,12},{1,17},{... | collective-permute-start | bytes 344072 | tf_op jit(solution)/shard_map/ppermute | solution.py:270
  136.5 5.4 %collective-permute-done.16 = bf16[448,384]{1,0:T(8,128)(2,1)S(1)} collective-permute-done((bf16[448,384]{1,0:T(8,128)(2,1)S(1)}, bf16[448,384]{1,0:T(8,128)(2,1)S(1)}, u32[]{:S(2)}, u32[]{:S(2)}) %collective-permute-start.16) | collective-permute-done | bytes 344096 | tf_op jit(solution)/shard_map/ppermute | solution.py:270
  141.9 0.1 convert_add_fusion.1
  142.0 1.7 %collective-permute-start.17 = (bf16[224,384]{1,0:T(8,128)(2,1)S(1)}, bf16[224,384]{1,0:T(8,128)(2,1)S(1)}, u32[]{:S(2)}, u32[]{:S(2)}) collective-permute-start(bf16[224,384]{1,0:T(8,128)(2,1)S(1)} %slice.40), channel_id=1, source_target_pairs={{0,16},{4,20},{8,24},{12,28},{16,0},{20,4},{24,8},{28,12},{1,17},{... | collective-permute-start | bytes 516104 | tf_op jit(solution)/shard_map/ppermute | solution.py:270
  143.7 8.1 %collective-permute-done.21 = bf16[448,384]{1,0:T(8,128)(2,1)S(1)} collective-permute-done((bf16[448,384]{1,0:T(8,128)(2,1)}, bf16[448,384]{1,0:T(8,128)(2,1)S(1)}, u32[]{:S(2)}, u32[]{:S(2)}) %collective-permute-start.21) | collective-permute-done | bytes 344096 | tf_op jit(solution)/shard_map/ppermute | solution.py:270
  151.8 0.1 convert_add_fusion
  151.9 0.3 collective-permute-start.22
  152.3 6.2 %collective-permute-done.17 = bf16[224,384]{1,0:T(8,128)(2,1)S(1)} collective-permute-done((bf16[224,384]{1,0:T(8,128)(2,1)S(1)}, bf16[224,384]{1,0:T(8,128)(2,1)S(1)}, u32[]{:S(2)}, u32[]{:S(2)}) %collective-permute-start.17) | collective-permute-done | bytes 172064 | tf_op jit(solution)/shard_map/ppermute | solution.py:270
  158.5 3.4 %collective-permute-done.22 = bf16[224,384]{1,0:T(8,128)(2,1)S(1)} collective-permute-done((bf16[224,384]{1,0:T(8,128)(2,1)S(1)}, bf16[224,384]{1,0:T(8,128)(2,1)S(1)}, u32[]{:S(2)}, u32[]{:S(2)}) %collective-permute-start.22) | collective-permute-done | bytes 172064 | tf_op jit(solution)/shard_map/ppermute | solution.py:270
  161.9 1.0 maximum_multiply_fusion
  (46 shorter events, 0.3 us)
Async XLA Ops:
  0.6 2.4 %copy-start.10 = (s32[8]{0:T(128)S(1)}, s32[8]{0:T(128)}, u32[]{:S(2)}) copy-start(s32[8]{0:T(128)} %constant.58.clone) | copy-start | bytes 100
  0.6 14.9 %copy-start = (bf16[1,384,4096]{2,1,0:T(8,128)(2,1)S(1)}, bf16[1,384,4096]{2,1,0:T(8,128)(2,1)}, u32[]{:S(2)}) copy-start(bf16[1,384,4096]{2,1,0:T(8,128)(2,1)} %param.4) | copy-start | bytes 9437188
  7.8 4.9 %collective-permute-start.3 = (f32[1,5888]{1,0:T(1,128)S(1)}, f32[1,5888]{1,0:T(1,128)S(1)}, u32[]{:S(2)}, u32[]{:S(2)}) collective-permute-start(f32[1,5888]{1,0:T(1,128)S(1)} %pad_maximum_fusion), channel_id=1, source_target_pairs={{0,4},{4,0},{8,12},{12,8},{16,20},{20,16},{24,28},{28,24},{1,5},{5... | collective-permute-start | bytes 70664 | tf_op jit(solution)/shard_map/ppermute | solution.py:270
  10.9 18.6 %collective-permute-start.1 = (bf16[896,384]{1,0:T(8,128)(2,1)}, bf16[896,384]{1,0:T(8,128)(2,1)}, u32[]{:S(2)}, u32[]{:S(2)}) collective-permute-start(bf16[896,384]{1,0:T(8,128)(2,1)} %get-tuple-element.22.refs_0_), channel_id=1, source_target_pairs={{0,2},{1,3},{2,0},{3,1},{4,6},{5,7},{6,4},{7,5},{8,10},{9,11},{10,... | collective-permute-start | bytes 2064392 | tf_op jit(solution)/shard_map/ppermute | solution.py:270
  12.4 32.5 %collective-permute-start = (bf16[896,384]{1,0:T(8,128)(2,1)}, bf16[896,384]{1,0:T(8,128)(2,1)}, u32[]{:S(2)}, u32[]{:S(2)}) collective-permute-start(bf16[896,384]{1,0:T(8,128)(2,1)} %get-tuple-element.22.refs_0_), channel_id=1, source_target_pairs={{0,1},{1,0},{2,3},{3,2},{4,5},{5,4},{6,7},{7,6},{8,9},{9,8},{10,11... | collective-permute-start | bytes 2064392 | tf_op jit(solution)/shard_map/ppermute | solution.py:270
  13.4 28.1 %copy-start.8 = (s32[8]{0:T(128)S(1)}, s32[8]{0:T(128)}, u32[]{:S(2)}) copy-start(s32[8]{0:T(128)} %broadcast_xor_fusion.order) | copy-start | bytes 100
  13.4 4.6 %collective-permute-start.4 = (f32[1,5888]{1,0:T(1,128)S(1)}, f32[1,5888]{1,0:T(1,128)S(1)}, u32[]{:S(2)}, u32[]{:S(2)}) collective-permute-start(f32[1,5888]{1,0:T(1,128)S(1)} %fusion.8), channel_id=1, source_target_pairs={{0,8},{4,12},{8,0},{12,4},{16,24},{20,28},{24,16},{28,20},{1,9},{5... | collective-permute-start | bytes 70664 | tf_op jit(solution)/shard_map/ppermute | solution.py:270
  16.5 24.8 %collective-permute-start.10 = (bf16[384,384]{1,0:T(8,128)(2,1)}, bf16[384,384]{1,0:T(8,128)(2,1)}, u32[]{:S(2)}, u32[]{:S(2)}) collective-permute-start(bf16[384,384]{1,0:T(8,128)(2,1)} %get-tuple-element.43), channel_id=1, source_target_pairs={{0,2},{1,3},{2,0},{3,1},{4,6},{5,7},{6,4},{7,5},{8,10},{9,11},{10,... | collective-permute-start | bytes 884744 | tf_op jit(solution)/shard_map/ppermute | solution.py:270
  18.1 11.5 %collective-permute-start.5 = (f32[1,5888]{1,0:T(1,128)S(1)}, f32[1,5888]{1,0:T(1,128)S(1)}, u32[]{:S(2)}, u32[]{:S(2)}) collective-permute-start(f32[1,5888]{1,0:T(1,128)S(1)} %max.16), channel_id=1, source_target_pairs={{0,16},{4,20},{8,24},{12,28},{16,0},{20,4},{24,8},{28,12},{1,17},{... | collective-permute-start | bytes 70664 | tf_op jit(solution)/shard_map/ppermute | solution.py:270
  22.0 42.0 %collective-permute-start.9 = (bf16[384,1024]{1,0:T(8,128)(2,1)}, bf16[384,1024]{1,0:T(8,128)(2,1)}, u32[]{:S(2)}, u32[]{:S(2)}) collective-permute-start(bf16[384,1024]{1,0:T(8,128)(2,1)} %get-tuple-element.46), channel_id=1, source_target_pairs={{0,1},{1,0},{2,3},{3,2},{4,5},{5,4},{6,7},{7,6},{8,9},{9,8},{10,11... | collective-permute-start | bytes 2359304 | tf_op jit(solution)/shard_map/ppermute | solution.py:270
  29.5 16.0 %collective-permute-start.2 = (bf16[896,384]{1,0:T(8,128)(2,1)}, bf16[896,384]{1,0:T(8,128)(2,1)}, u32[]{:S(2)}, u32[]{:S(2)}) collective-permute-start(bf16[896,384]{1,0:T(8,128)(2,1)} %collective-permute-done.1.refs_2_), channel_id=1, source_target_pairs={{0,1},{1,0},{2,3},{3,2},{4,5},{5,4},{6,7},{7,6},{8,9},{9,8},{10,11... | collective-permute-start | bytes 2064392 | tf_op jit(solution)/shard_map/ppermute | solution.py:270
  29.6 12.6 %copy-start.4 = (f32[1,5888]{1,0:T(1,128)}, f32[1,5888]{1,0:T(1,128)S(1)}, u32[]{:S(2)}) copy-start(f32[1,5888]{1,0:T(1,128)S(1)} %maximum_maximum_fusion.refs_0_) | copy-start | bytes 70660
  29.6 2.4 %collective-permute-start.6 = (f32[1,5888]{1,0:T(1,128)S(1)}, f32[1,5888]{1,0:T(1,128)S(1)}, u32[]{:S(2)}, u32[]{:S(2)}) collective-permute-start(f32[1,5888]{1,0:T(1,128)S(1)} %maximum_maximum_fusion.refs_0_), channel_id=1, source_target_pairs={{0,1},{1,0},{2,3},{3,2},{4,5},{5,4},{6,7},{7,6},{8,9},{9,8},{10,11... | collective-permute-start | bytes 70664 | tf_op jit(solution)/shard_map/ppermute | solution.py:270
  32.0 10.1 %copy-start.5 = (f32[1,5888]{1,0:T(1,128)}, f32[1,5888]{1,0:T(1,128)S(1)}, u32[]{:S(2)}) copy-start(f32[1,5888]{1,0:T(1,128)S(1)} %collective-permute-done.6.refs_1_) | copy-start | bytes 70660
  32.0 3.8 %collective-permute-start.7 = (f32[1,5888]{1,0:T(1,128)S(1)}, f32[1,5888]{1,0:T(1,128)S(1)}, u32[]{:S(2)}, u32[]{:S(2)}) collective-permute-start(f32[1,5888]{1,0:T(1,128)S(1)} %maximum_maximum_fusion.refs_0_), channel_id=1, source_target_pairs={{0,2},{1,3},{2,0},{3,1},{4,6},{5,7},{6,4},{7,5},{8,10},{9,11},{10,... | collective-permute-start | bytes 70664 | tf_op jit(solution)/shard_map/ppermute | solution.py:270
  35.8 6.3 %copy-start.6 = (f32[1,5888]{1,0:T(1,128)}, f32[1,5888]{1,0:T(1,128)S(1)}, u32[]{:S(2)}) copy-start(f32[1,5888]{1,0:T(1,128)S(1)} %collective-permute-done.7.refs_2_) | copy-start | bytes 70660
  35.8 3.4 %collective-permute-start.8 = (f32[1,5888]{1,0:T(1,128)S(1)}, f32[1,5888]{1,0:T(1,128)S(1)}, u32[]{:S(2)}, u32[]{:S(2)}) collective-permute-start(f32[1,5888]{1,0:T(1,128)S(1)} %maximum_maximum_fusion.refs_0_), channel_id=1, source_target_pairs={{0,3},{1,2},{2,1},{3,0},{4,7},{5,6},{6,5},{7,4},{8,11},{9,10},{10,... | collective-permute-start | bytes 70664 | tf_op jit(solution)/shard_map/ppermute | solution.py:270
  39.3 2.9 %copy-start.7 = (f32[1,5888]{1,0:T(1,128)}, f32[1,5888]{1,0:T(1,128)S(1)}, u32[]{:S(2)}) copy-start(f32[1,5888]{1,0:T(1,128)S(1)} %collective-permute-done.8.refs_3_) | copy-start | bytes 70660
  39.3 32.0 %collective-permute-start.14 = (bf16[896,384]{1,0:T(8,128)(2,1)}, bf16[896,384]{1,0:T(8,128)(2,1)}, u32[]{:S(2)}, u32[]{:S(2)}) collective-permute-start(bf16[896,384]{1,0:T(8,128)(2,1)} %get-tuple-element.28.refs_2_), channel_id=1, source_target_pairs={{0,2},{1,3},{2,0},{3,1},{4,6},{5,7},{6,4},{7,5},{8,10},{9,11},{10,... | collective-permute-start | bytes 2064392 | tf_op jit(solution)/shard_map/ppermute | solution.py:270
  41.4 21.7 %collective-permute-start.11 = (bf16[384,384]{1,0:T(8,128)(2,1)}, bf16[384,384]{1,0:T(8,128)(2,1)}, u32[]{:S(2)}, u32[]{:S(2)}) collective-permute-start(bf16[384,384]{1,0:T(8,128)(2,1)} %get-tuple-element.42), channel_id=1, source_target_pairs={{0,3},{1,2},{2,1},{3,0},{4,7},{5,6},{6,5},{7,4},{8,11},{9,10},{10,... | collective-permute-start | bytes 884744 | tf_op jit(solution)/shard_map/ppermute | solution.py:270
  44.9 26.3 %collective-permute-start.18 = (bf16[384,384]{1,0:T(8,128)(2,1)}, bf16[384,384]{1,0:T(8,128)(2,1)}, u32[]{:S(2)}, u32[]{:S(2)}) collective-permute-start(bf16[384,384]{1,0:T(8,128)(2,1)} %get-tuple-element.41), channel_id=1, source_target_pairs={{0,2},{1,3},{2,0},{3,1},{4,6},{5,7},{6,4},{7,5},{8,10},{9,11},{10,... | collective-permute-start | bytes 884744 | tf_op jit(solution)/shard_map/ppermute | solution.py:270
  45.5 30.1 %collective-permute-start.19 = (bf16[384,384]{1,0:T(8,128)(2,1)S(1)}, bf16[384,384]{1,0:T(8,128)(2,1)}, u32[]{:S(2)}, u32[]{:S(2)}) collective-permute-start(bf16[384,384]{1,0:T(8,128)(2,1)S(1)} %get-tuple-element.40), channel_id=1, source_target_pairs={{0,3},{1,2},{2,1},{3,0},{4,7},{5,6},{6,5},{7,4},{8,11},{9,10},{10,... | collective-permute-start | bytes 884744 | tf_op jit(solution)/shard_map/ppermute | solution.py:270
  63.0 37.2 %collective-permute-start.13 = (bf16[896,384]{1,0:T(8,128)(2,1)}, bf16[896,384]{1,0:T(8,128)(2,1)}, u32[]{:S(2)}, u32[]{:S(2)}) collective-permute-start(bf16[896,384]{1,0:T(8,128)(2,1)} %get-tuple-element.28.refs_2_), channel_id=1, source_target_pairs={{0,1},{1,0},{2,3},{3,2},{4,5},{5,4},{6,7},{7,6},{8,9},{9,8},{10,11... | collective-permute-start | bytes 2064392 | tf_op jit(solution)/shard_map/ppermute | solution.py:270
  64.1 17.9 %collective-permute-start.23 = (bf16[384,256]{1,0:T(8,128)(2,1)}, bf16[384,256]{1,0:T(8,128)(2,1)}, u32[]{:S(2)}, u32[]{:S(2)}) collective-permute-start(bf16[384,256]{1,0:T(8,128)(2,1)} %get-tuple-element.45), channel_id=1, source_target_pairs={{0,2},{1,3},{2,0},{3,1},{4,6},{5,7},{6,4},{7,5},{8,10},{9,11},{10,... | collective-permute-start | bytes 589832 | tf_op jit(solution)/shard_map/ppermute | solution.py:270
  71.2 12.3 %collective-permute-start.24 = (bf16[384,256]{1,0:T(8,128)(2,1)}, bf16[384,256]{1,0:T(8,128)(2,1)}, u32[]{:S(2)}, u32[]{:S(2)}) collective-permute-start(bf16[384,256]{1,0:T(8,128)(2,1)} %get-tuple-element.44), channel_id=1, source_target_pairs={{0,3},{1,2},{2,1},{3,0},{4,7},{5,6},{6,5},{7,4},{8,11},{9,10},{10,... | collective-permute-start | bytes 589832 | tf_op jit(solution)/shard_map/ppermute | solution.py:270
  71.3 28.9 %collective-permute-start.15 = (bf16[896,384]{1,0:T(8,128)(2,1)}, bf16[896,384]{1,0:T(8,128)(2,1)}, u32[]{:S(2)}, u32[]{:S(2)}) collective-permute-start(bf16[896,384]{1,0:T(8,128)(2,1)} %collective-permute-done.14.refs_4_), channel_id=1, source_target_pairs={{0,1},{1,0},{2,3},{3,2},{4,5},{5,4},{6,7},{7,6},{8,9},{9,8},{10,11... | collective-permute-start | bytes 2064392 | tf_op jit(solution)/shard_map/ppermute | solution.py:270
  75.6 24.7 %collective-permute-start.12 = (bf16[896,384]{1,0:T(8,128)(2,1)}, bf16[896,384]{1,0:T(8,128)(2,1)}, u32[]{:S(2)}, u32[]{:S(2)}) collective-permute-start(bf16[896,384]{1,0:T(8,128)(2,1)} %get-tuple-element.27), channel_id=1, source_target_pairs={{0,4},{4,0},{8,12},{12,8},{16,20},{20,16},{24,28},{28,24},{1,5},{5... | collective-permute-start | bytes 2064392 | tf_op jit(solution)/shard_map/ppermute | solution.py:270
  82.0 44.8 %collective-permute-start.20 = (bf16[896,384]{1,0:T(8,128)(2,1)}, bf16[896,384]{1,0:T(8,128)(2,1)}, u32[]{:S(2)}, u32[]{:S(2)}) collective-permute-start(bf16[896,384]{1,0:T(8,128)(2,1)} %get-tuple-element.32), channel_id=1, source_target_pairs={{0,4},{4,0},{8,12},{12,8},{16,20},{20,16},{24,28},{28,24},{1,5},{5... | collective-permute-start | bytes 2064392 | tf_op jit(solution)/shard_map/ppermute | solution.py:270
  88.2 30.4 %collective-permute-start.25 = (bf16[896,256]{1,0:T(8,128)(2,1)}, bf16[896,256]{1,0:T(8,128)(2,1)}, u32[]{:S(2)}, u32[]{:S(2)}) collective-permute-start(bf16[896,256]{1,0:T(8,128)(2,1)} %get-tuple-element.37), channel_id=1, source_target_pairs={{0,4},{4,0},{8,12},{12,8},{16,20},{20,16},{24,28},{28,24},{1,5},{5... | collective-permute-start | bytes 1376264 | tf_op jit(solution)/shard_map/ppermute | solution.py:270
  108.9 17.4 %copy-start.9 = (bf16[448,384]{1,0:T(8,128)(2,1)S(1)}, bf16[448,384]{1,0:T(8,128)(2,1)}, u32[]{:S(2)}) copy-start(bf16[448,384]{1,0:T(8,128)(2,1)} %get-tuple-element.30) | copy-start | bytes 1032196
  123.4 10.4 %collective-permute-start.26 = (bf16[448,256]{1,0:T(8,128)(2,1)}, bf16[448,256]{1,0:T(8,128)(2,1)S(1)}, u32[]{:S(2)}, u32[]{:S(2)}) collective-permute-start(bf16[448,256]{1,0:T(8,128)(2,1)} %get-tuple-element.39), channel_id=1, source_target_pairs={{0,8},{4,12},{8,0},{12,4},{16,24},{20,28},{24,16},{28,20},{1,9},{5... | collective-permute-start | bytes 688136 | tf_op jit(solution)/shard_map/ppermute | solution.py:270
  126.2 15.7 %collective-permute-start.16 = (bf16[448,384]{1,0:T(8,128)(2,1)S(1)}, bf16[448,384]{1,0:T(8,128)(2,1)S(1)}, u32[]{:S(2)}, u32[]{:S(2)}) collective-permute-start(bf16[448,384]{1,0:T(8,128)(2,1)S(1)} %copy-done.9), channel_id=1, source_target_pairs={{0,8},{4,12},{8,0},{12,4},{16,24},{20,28},{24,16},{28,20},{1,9},{5... | collective-permute-start | bytes 1032200 | tf_op jit(solution)/shard_map/ppermute | solution.py:270
  126.7 7.0 %copy-start.3 = (f32[448,256]{1,0:T(8,128)S(1)}, f32[448,256]{1,0:T(8,128)}, u32[]{:S(2)}) copy-start(f32[448,256]{1,0:T(8,128)} %get-tuple-element.38) | copy-start | bytes 1376260
  126.7 15.2 %copy-start.1 = (f32[448,384]{1,0:T(8,128)S(1)}, f32[448,384]{1,0:T(8,128)}, u32[]{:S(2)}) copy-start(f32[448,384]{1,0:T(8,128)} %get-tuple-element.29) | copy-start | bytes 2064388
  132.2 19.6 %copy-start.2 = (f32[448,384]{1,0:T(8,128)S(1)}, f32[448,384]{1,0:T(8,128)}, u32[]{:S(2)}) copy-start(f32[448,384]{1,0:T(8,128)} %get-tuple-element.34) | copy-start | bytes 2064388
  132.2 19.6 %collective-permute-start.21 = (bf16[448,384]{1,0:T(8,128)(2,1)}, bf16[448,384]{1,0:T(8,128)(2,1)S(1)}, u32[]{:S(2)}, u32[]{:S(2)}) collective-permute-start(bf16[448,384]{1,0:T(8,128)(2,1)} %get-tuple-element.35), channel_id=1, source_target_pairs={{0,8},{4,12},{8,0},{12,4},{16,24},{20,28},{24,16},{28,20},{1,9},{5... | collective-permute-start | bytes 1032200 | tf_op jit(solution)/shard_map/ppermute | solution.py:270
  133.8 18.4 %collective-permute-start.27 = (bf16[224,256]{1,0:T(8,128)(2,1)S(1)}, bf16[224,256]{1,0:T(8,128)(2,1)S(1)}, u32[]{:S(2)}, u32[]{:S(2)}) collective-permute-start(bf16[224,256]{1,0:T(8,128)(2,1)S(1)} %slice.41), channel_id=1, source_target_pairs={{0,16},{4,20},{8,24},{12,28},{16,0},{20,4},{24,8},{28,12},{1,17},{... | collective-permute-start | bytes 344072 | tf_op jit(solution)/shard_map/ppermute | solution.py:270
  142.0 16.5 %collective-permute-start.17 = (bf16[224,384]{1,0:T(8,128)(2,1)S(1)}, bf16[224,384]{1,0:T(8,128)(2,1)S(1)}, u32[]{:S(2)}, u32[]{:S(2)}) collective-permute-start(bf16[224,384]{1,0:T(8,128)(2,1)S(1)} %slice.40), channel_id=1, source_target_pairs={{0,16},{4,20},{8,24},{12,28},{16,0},{20,4},{24,8},{28,12},{1,17},{... | collective-permute-start | bytes 516104 | tf_op jit(solution)/shard_map/ppermute | solution.py:270
  151.9 10.0 %collective-permute-start.22 = (bf16[224,384]{1,0:T(8,128)(2,1)S(1)}, bf16[224,384]{1,0:T(8,128)(2,1)S(1)}, u32[]{:S(2)}, u32[]{:S(2)}) collective-permute-start(bf16[224,384]{1,0:T(8,128)(2,1)S(1)} %slice.39), channel_id=1, source_target_pairs={{0,16},{4,20},{8,24},{12,28},{16,0},{20,4},{24,8},{28,12},{1,17},{... | collective-permute-start | bytes 516104 | tf_op jit(solution)/shard_map/ppermute | solution.py:270

commit v2 on v1

--- a/solution.py
+++ b/solution.py
@@ -8,6 +8,7 @@
 
 ceiling = 448.0
 LANES = 128
+PARAMS = pltpu.CompilerParams(vmem_limit_bytes=24 * 2**20)
 
 
 def to_grid(values, factor, scale):
@@ -31,13 +32,13 @@
     return order
 
 
-def turn_rows(hdata, blocks, ctx_count):
+def turn_rows(hdata, where_to, ctx_count):
     tokens, ff = hdata.shape
     rows = ff // ctx_count
     wide = ff // 2 if (ff // 2) % LANES == 0 else LANES
     steps = ff // wide
 
-    def body(order, source, sent, kept, peaks, turned):
+    def body(where_ref, source, sent, kept, peaks, turned):
         step = pl.program_id(0)
         tile = source[...]
         peaks[...] = jnp.max(jnp.abs(tile.astype(jnp.float32)), axis=0, keepdims=True)
@@ -47,7 +48,7 @@
         def _():
             for half, target in enumerate((sent, kept)):
                 for j in range(ctx_count // 2):
-                    block = order[half * (ctx_count // 2) + j]
+                    block = where_ref[0] ^ row_order(ctx_count)[half * (ctx_count // 2) + j]
                     start = pl.multiple_of(block * rows, 16)
                     target[j * rows : (j + 1) * rows, :] = turned[pl.ds(start, rows), :]
 
@@ -66,8 +67,71 @@
             ],
             scratch_shapes=[pltpu.VMEM((ff, tokens), jnp.bfloat16)],
         ),
+        compiler_params=PARAMS,
         name="turn_rows",
-    )(blocks, hdata)
+    )(where_to, hdata)
+
+
+def split_columns(gdata, where_to, dp_count, sizes):
+    tokens, width = gdata.shape
+    own_cols = width // dp_count
+    shapes = [(tokens, own_cols)] * 2 + [(tokens, size) for _ in range(2, dp_count) for size in sizes]
+
+    def body(where_ref, source, *refs):
+        peaks, outs = refs[-1], refs[:-1]
+        tile = source[...]
+        peaks[...] = jnp.max(jnp.abs(tile.astype(jnp.float32)), axis=0, keepdims=True)
+        for k in range(dp_count):
+
+            @pl.when(pl.program_id(0) == k)
+            def _(k=k):
+                if k < 2:
+                    outs[k][...] = tile
+                    return
+                start = 0
+                for j, size in enumerate(sizes):
+                    outs[2 + (k - 2) * len(sizes) + j][...] = tile[:, start : start + size]
+                    start += size
+
+    by_distance = lambda i, w: (0, w[1] ^ i)
+    return pl.pallas_call(
+        body,
+        out_shape=[jax.ShapeDtypeStruct(shape, jnp.bfloat16) for shape in shapes]
+        + [jax.ShapeDtypeStruct((1, width), jnp.float32)],
+        grid_spec=pltpu.PrefetchScalarGridSpec(
+            num_scalar_prefetch=1,
+            grid=(dp_count,),
+            in_specs=[pl.BlockSpec((tokens, own_cols), by_distance)],
+            out_specs=[pl.BlockSpec(shape, lambda i, w: (0, 0)) for shape in shapes]
+            + [pl.BlockSpec((1, own_cols), by_distance)],
+        ),
+        compiler_params=PARAMS,
+        name="split_columns",
+    )(where_to, gdata)
+
+
+def input_gradient(gdata, down_weight):
+    tokens, width = gdata.shape
+    ff = down_weight.shape[0]
+    tile = 256 if ff % 256 == 0 else LANES
+
+    def body(left, right, out):
+        out[...] = lax.dot_general(
+            left[...], right[...], (((1,), (1,)), ((), ())), preferred_element_type=jnp.float32
+        ).astype(jnp.bfloat16)
+
+    return pl.pallas_call(
+        body,
+        out_shape=jax.ShapeDtypeStruct((tokens, ff), jnp.bfloat16),
+        grid=(ff // tile,),
+        in_specs=[pl.BlockSpec((tokens, width), lambda i: (0, 0)), pl.BlockSpec((tile, width), lambda i: (i, 0))],
+        out_specs=pl.BlockSpec((tokens, tile), lambda i: (0, i)),
+        cost_estimate=pl.CostEstimate(
+            flops=2 * tokens * width * ff, transcendentals=0, bytes_accessed=2 * width * (tokens + ff)
+        ),
+        compiler_params=PARAMS,
+        name="input_gradient",
+    )(gdata, down_weight)
 
 
 def divide(peak):
@@ -81,10 +145,19 @@
 def scale_tables(peaks, where_to, ff, own_cols, ctx_count):
     count = len(peaks)
     rows = ff // ctx_count
+    width_cols = (peaks[0].shape[1] - ff) // ctx_count
 
     def body(where_ref, *refs):
-        sources, (cols, gtable), (by_lane, by_row) = refs[:count], refs[count : count + 2], refs[count + 2 :]
-        start = pl.multiple_of(ff + where_ref[ctx_count] * own_cols, LANES)
+        sources, rest = refs[:count], refs[count:]
+        cols, gtable, hidden_amax, grad_amax, by_lane, by_row = rest
+        for out, base in ((hidden_amax, 0), (grad_amax, ff)):
+            size = out.shape[1]
+            picked = sources[0][:, base : base + size]
+            for j in range(1, ctx_count):
+                other = sources[0][:, base + j * size : base + (j + 1) * size]
+                picked = jnp.where(where_ref[0] == j, other, picked)
+            out[...] = picked
+        start = pl.multiple_of(ff + where_ref[1] * own_cols, LANES)
         for r in range(count):
             peak = sources[r][:, :ff]
             by_lane[r : r + 1, :] = divide(peak)
@@ -95,7 +168,7 @@
         for c in range(0, ff, LANES):
             by_row[c : c + LANES, :] = by_lane[:, c : c + LANES].T
         for j in range(ctx_count):
-            begin = pl.multiple_of(where_ref[j] * rows, 8)
+            begin = pl.multiple_of((where_ref[0] ^ row_order(ctx_count)[j]) * rows, 8)
             cols[j * rows : (j + 1) * rows, :] = by_row[pl.ds(begin, rows), :]
 
     whole = lambda i, w: (0, 0)
@@ -104,39 +177,48 @@
         out_shape=(
             jax.ShapeDtypeStruct((ff, 2 * count), jnp.float32),
             jax.ShapeDtypeStruct((2 * count, own_cols), jnp.float32),
+            jax.ShapeDtypeStruct((1, rows), jnp.float32),
+            jax.ShapeDtypeStruct((1, width_cols), jnp.float32),
         ),
         grid_spec=pltpu.PrefetchScalarGridSpec(
             num_scalar_prefetch=1,
             grid=(1,),
             in_specs=[pl.BlockSpec(peaks[0].shape, whole)] * count,
-            out_specs=[pl.BlockSpec((ff, 2 * count), whole), pl.BlockSpec((2 * count, own_cols), whole)],
+            out_specs=[
+                pl.BlockSpec((ff, 2 * count), whole),
+                pl.BlockSpec((2 * count, own_cols), whole),
+                pl.BlockSpec((1, rows), whole),
+                pl.BlockSpec((1, width_cols), whole),
+            ],
             scratch_shapes=[pltpu.VMEM((2 * count, ff), jnp.float32), pltpu.VMEM((ff, 2 * count), jnp.float32)],
         ),
+        compiler_params=PARAMS,
         name="scale_tables",
     )(where_to, *peaks)
 
 
-def quantize_rows(sources, cols, offset, tile):
+def quantize_rows(sources, cols, tile):
     rows, tokens = sources[0].shape
     count = len(sources)
 
     def body(*refs):
-        cols_ref, out = refs[count], refs[count + 1]
+        cols_ref, out = refs[count:]
         for r in range(count):
             out[:, r * tokens : (r + 1) * tokens] = to_grid(
                 refs[r][...], cols_ref[:, r : r + 1], cols_ref[:, count + r : count + r + 1]
             )
 
+    by_step = lambda i: (i, 0)
     return pl.pallas_call(
         body,
         out_shape=jax.ShapeDtypeStruct((rows, count * tokens), jnp.bfloat16),
         grid=(rows // tile,),
-        in_specs=[pl.BlockSpec((tile, tokens), lambda i: (i, 0))] * count
-        + [pl.BlockSpec((tile, 2 * count), lambda i: (i + offset // tile, 0))],
-        out_specs=pl.BlockSpec((tile, count * tokens), lambda i: (i, 0)),
+        in_specs=[pl.BlockSpec((tile, tokens), by_step)] * count + [pl.BlockSpec((tile, 2 * count), by_step)],
+        out_specs=pl.BlockSpec((tile, count * tokens), by_step),
         cost_estimate=pl.CostEstimate(
             flops=2000 * rows * tokens * count, transcendentals=0, bytes_accessed=4 * rows * tokens * count
         ),
+        compiler_params=PARAMS,
         name="quantize_rows",
     )(*sources, cols)
 
@@ -180,6 +262,7 @@
         cost_estimate=pl.CostEstimate(
             flops=4 * rows * depth * width, transcendentals=0, bytes_accessed=2 * depth * (rows + width)
         ),
+        compiler_params=PARAMS,
         name="quantize_and_multiply",
     )(hq, gtable, *sources)
 
@@ -242,15 +325,18 @@
         cost_estimate=pl.CostEstimate(
             flops=4 * rows * depth * width, transcendentals=0, bytes_accessed=2 * depth * (rows + width)
         ),
+        compiler_params=PARAMS,
         name="finish",
     )(*operands)
 
 
-def split_width(width, parts):
+SHARES = (0.375, 0.625, 0.875, 1.0)
+
+
+def split_width(width):
     units = width // LANES
-    parts = min(parts, units)
-    sizes = [units // parts + (1 if i < units % parts else 0) for i in range(parts)]
-    return [size * LANES for size in sizes]
+    ends = [0] + [round(units * share) for share in SHARES]
+    return [(end - begin) * LANES for begin, end in zip(ends, ends[1:]) if end > begin]
 
 
 def on_device(grad_out, hidden, down_weight):
@@ -260,7 +346,7 @@
     ctx_count, dp_count = lax.axis_size("ctx"), lax.axis_size("dp")
     position, place = lax.axis_index("ctx"), lax.axis_index("dp")
     ff, width = hdata.shape[1], gdata.shape[1]
-    ff_rows, width_cols = ff // ctx_count, width // ctx_count
+    ff_rows = ff // ctx_count
     own_cols = width // dp_count
     seq_total = tokens * ctx_count * dp_count
     tile = 2 * ff_rows
@@ -269,23 +355,17 @@
         count = ctx_count if axis == "ctx" else dp_count
         return lax.ppermute(value, axis, [(i, i ^ distance) for i in range(count)])
 
-    sizes = split_width(own_cols, 3)
+    sizes = split_width(own_cols)
     starts = [sum(sizes[:j]) for j in range(len(sizes))]
 
-    def column_block(k, start, size):
-        return lax.dynamic_slice(gdata, (0, (place ^ k) * own_cols + start), (tokens, size))
-
-    own_block = column_block(0, 0, own_cols)
-    near_block = swap(column_block(1, 0, own_cols), "dp", 1)
+    where_to = jnp.stack([position, place]).astype(jnp.int32)
+    sent_rows, kept_rows, hpeak = turn_rows(hdata, where_to, ctx_count)
+    own_block, near_block, *far_blocks, gpeak = split_columns(gdata, where_to, dp_count, sizes)
+    near_block = swap(near_block, "dp", 1)
     chunks = []
-    for start, size in zip(starts, sizes):
-        parts = [own_block, near_block]
-        for k in range(2, dp_count):
-            parts.append(swap(column_block(k, start, size), "dp", k))
-        chunks.append(parts)
-
-    blocks = position ^ jnp.array(row_order(ctx_count), jnp.int32)
-    sent_rows, kept_rows, hpeak = turn_rows(hdata, blocks, ctx_count)
+    for j in range(len(sizes)):
+        far = [swap(far_blocks[(k - 2) * len(sizes) + j], "dp", k) for k in range(2, dp_count)]
+        chunks.append([own_block, near_block] + far)
 
     def spread(value):
         slots = [value, swap(value, "dp", 1)]
@@ -297,25 +377,23 @@
     sent_slots = spread(sent_rows)
     kept_slots = spread(kept_rows)
 
-    gpeak = jnp.max(jnp.abs(gdata.astype(jnp.float32)), axis=0, keepdims=True)
     peaks = jnp.concatenate([hpeak, gpeak], axis=1)
     bit = 1
     while bit < ctx_count:
         peaks = jnp.maximum(peaks, swap(peaks, "ctx", bit))
         bit *= 2
     peaks = jnp.maximum(peaks, 1.0)
-    hidden_amax = lax.dynamic_slice(peaks, (0, position * ff_rows), (1, ff_rows))
-    grad_amax = lax.dynamic_slice(peaks, (0, ff + position * width_cols), (1, width_cols))
     all_peaks = [peaks] + [swap(peaks, "dp", k) for k in range(1, dp_count)]
-    where_to = jnp.concatenate([blocks, place[None]])
-    cols, gtable = scale_tables(all_peaks, where_to, ff, own_cols, ctx_count)
-    hq_sent = quantize_rows(sent_slots, cols, 0, ff_rows)
-    rows_in, results = kept_slots, []
+    cols, gtable, hidden_amax, grad_amax = scale_tables(
+        all_peaks, where_to, ff, own_cols, ctx_count
+    )
+    hq_sent = quantize_rows(sent_slots, cols, ff_rows)
+    kept_in, results = kept_slots, []
     for j, (start, size) in enumerate(zip(starts, sizes)):
         outgoing, gq = quantize_and_multiply(hq_sent, chunks[j], gtable, start, tile)
         arrived = swap(outgoing, "ctx", 1)
-        send, keep, *quantized = finish(rows_in, cols, gq, arrived, ff_rows)
-        rows_in = quantized[0] if quantized else rows_in
+        send, keep, *quantized = finish(kept_in, cols, gq, arrived, ff_rows)
+        kept_in = quantized[0] if quantized else kept_in
         bit = 2
         while True:
             arrived = swap(send, "ctx", bit)
@@ -328,10 +406,7 @@
         results.append(total)
     weight_grad = jnp.concatenate(results, axis=1) / jnp.sqrt(jnp.float32(seq_total))
 
-    result = lax.dot_general(
-        gdata, down_weight, (((1,), (1,)), ((), ())), preferred_element_type=jnp.float32
-    )
-    grad_hidden = result.astype(jnp.bfloat16)[None]
+    grad_hidden = input_gradient(gdata, down_weight)[None]
     return (grad_hidden, weight_grad, hidden_amax, grad_amax)
 
 

time: 164 us -> 134 us (0.82)
  Pallas kernels: 48 us -> 34.6 us
  matrix products: 10.4 us -> 0 us
  starting transfers between devices: 30.4 us -> 35.7 us
  other arithmetic: 6.28 us -> 1.46 us
  waiting for transfers between devices: 61.4 us -> 57.6 us
  local copies, waits for them, and re-layouts: 5.67 us -> 3.31 us
    dot_general x1 -> x0, matrix products: 10.4 us -> none  [on_device(): lax.dot_general(gdata, down_weight, (((1,), (1,)), ((), ())), preferred_e...]
    pallas_call x0 -> x2, Pallas kernels: none -> 9.34 us  [the longest x1 7.83 us: input_gradient(): pl.pallas_call(body, out_shape=jax.ShapeDtypeStruct((tokens, ff), jnp.bfl...]
    pallas_call x3 -> x4, Pallas kernels: 18.9 us -> 9.68 us  [finish(): pl.pallas_call(body, out_shape=out_shape, grid=(steps,), in_specs=in_spec...]
    pallas_call x3 -> x4, Pallas kernels: 16.4 us -> 8.74 us  [quantize_and_multiply(): pl.pallas_call(body, out_shape=(jax.ShapeDtypeStruct((rows, width), jnp.b...]
    dynamic_slice x5 -> x0, local copies, waits for them, and re-layouts: 5.56 us -> none  [the longest x3 3.04 us: column_block(): lax.dynamic_slice(gdata, (0, (place ^ k) * own_cols + start), (tokens, si...]
    ppermute x28 -> x33, starting transfers between devices: 30.4 us -> 35.7 us  [swap(): return lax.ppermute(value, axis, [(i, i ^ distance) for i in range(count)])]
    ppermute x28 -> x33, waiting for transfers between devices: 61.4 us -> 57.6 us  [swap(): return lax.ppermute(value, axis, [(i, i ^ distance) for i in range(count)])]
    unnamed x22 -> x9, local copies, waits for them, and re-layouts: 0.05 us -> 3.24 us
  transfers between devices with their start and end apart: 28 -> 33, of which waited for: 13 -> 17; matrix products, arithmetic and copies ran while one was open for 11% -> 0% of each run, Pallas kernels for 27% -> 25%
where the time goes in v2:
time: 134 us
  waiting for transfers between devices  57.6 us (43%)
  starting transfers between devices  35.7 us (27%)
  Pallas kernels  34.6 us (26%)
  local copies, waits for them, and re-layouts  3.31 us (2%)
  other arithmetic  1.46 us (1%)
    ppermute x33, waiting for transfers between devices, swap(): return lax.ppermute(value, axis, [(i, i ^ distance) for i in range(count)])  57.6 us
    ppermute x33, starting transfers between devices, swap(): return lax.ppermute(value, axis, [(i, i ^ distance) for i in range(count)])  35.7 us
    pallas_call x4, Pallas kernels, finish(): pl.pallas_call(body, out_shape=out_shape, grid=(steps,), in_specs=in_spec...  9.68 us
    pallas_call x4, Pallas kernels, quantize_and_multiply(): pl.pallas_call(body, out_shape=(jax.ShapeDtypeStruct((rows, width), jnp.b...  8.74 us
    pallas_call x1, Pallas kernels, input_gradient(): pl.pallas_call(body, out_shape=jax.ShapeDtypeStruct((tokens, ff), jnp.bfl...  7.83 us
    pallas_call x1, Pallas kernels, quantize_rows(): pl.pallas_call(body, out_shape=jax.ShapeDtypeStruct((rows, count * tokens...  3.73 us
    unnamed x9, local copies, waits for them, and re-layouts  3.24 us
  transfers between devices with their start and end apart: 33, of which 17 were waited for; matrix products, arithmetic and copies ran while one was open for 0% of the time, Pallas kernels for 25%

profile of v2, /device:TPU:0, one launch (start us, length us, event | category | flops | bytes accessed | tf_op | source)
XLA Modules:
  0.0 133.5 jit_solution(1628114762544541361)
XLA Ops:
  0.6 0.1 pad_add_fusion.where_ref
  0.7 1.3 %copy-done.2 = bf16[1,384,1792]{2,1,0:T(8,128)(2,1)S(1)} copy-done((bf16[1,384,1792]{2,1,0:T(8,128)(2,1)S(1)}, bf16[1,384,1792]{2,1,0:T(8,128)(2,1)}, u32[]{:S(2)}) %copy-start.2) | copy-done | bytes 1376280
  2.0 1.3 turn_rows.1
  3.4 3.0 %collective-permute-start.1 = (bf16[896,384]{1,0:T(8,128)(2,1)S(1)}, bf16[896,384]{1,0:T(8,128)(2,1)S(1)}, u32[]{:S(2)}, u32[]{:S(2)}) collective-permute-start(bf16[896,384]{1,0:T(8,128)(2,1)S(1)} %get-tuple-element.39.refs_0_), channel_id=1, source_target_pairs={{0,2},{1,3},{2,0},{3,1},{4,6},{5,7},{6,4},{7,5},{8,10},{9,11},{10,... | collective-permute-start | bytes 2064392 | tf_op jit(solution)/shard_map/ppermute | solution.py:356
  6.4 1.9 %copy-done = bf16[1,384,4096]{2,1,0:T(8,128)(2,1)S(1)} copy-done((bf16[1,384,4096]{2,1,0:T(8,128)(2,1)S(1)}, bf16[1,384,4096]{2,1,0:T(8,128)(2,1)}, u32[]{:S(2)}) %copy-start) | copy-done | bytes 3145752
  8.3 1.5 %split_columns.1 = (bf16[384,1024]{1,0:T(8,128)(2,1)S(1)}, bf16[384,1024]{1,0:T(8,128)(2,1)S(1)}, bf16[384,384]{1,0:T(8,128)(2,1)S(1)}, bf16[384,256]{1,0:T(8,12...) custom-call(s32[2]{0:T(128)S(1)} %pad_add_fusion.where_ref, ...), custom_call_target="tpu_custom_call" | custom-call | tf_op jit(solution)/shard_map/split_columns/pallas_call | solution.py:97
  9.8 1.6 %collective-permute-start.3 = (f32[1,5888]{1,0:T(1,128)S(1)}, f32[1,5888]{1,0:T(1,128)S(1)}, u32[]{:S(2)}, u32[]{:S(2)}) collective-permute-start(f32[1,5888]{1,0:T(1,128)S(1)} %constant_dynamic-update-slice_fusion), channel_id=1, source_target_pairs={{0,4},{4,0},{8,12},{12,8},{16,20},{20,16},{24,28},{28,24},{1,5},{5... | collective-permute-start | bytes 70664 | tf_op jit(solution)/shard_map/ppermute | solution.py:356
  11.4 2.3 %collective-permute-done.3 = f32[1,5888]{1,0:T(1,128)S(1)} collective-permute-done((f32[1,5888]{1,0:T(1,128)S(1)}, f32[1,5888]{1,0:T(1,128)S(1)}, u32[]{:S(2)}, u32[]{:S(2)}) %collective-permute-start.3) | collective-permute-done | bytes 23584 | tf_op jit(solution)/shard_map/ppermute | solution.py:356
  13.8 1.6 %collective-permute-start.4 = (f32[1,5888]{1,0:T(1,128)S(1)}, f32[1,5888]{1,0:T(1,128)S(1)}, u32[]{:S(2)}, u32[]{:S(2)}) collective-permute-start(f32[1,5888]{1,0:T(1,128)S(1)} %max.15), channel_id=1, source_target_pairs={{0,8},{4,12},{8,0},{12,4},{16,24},{20,28},{24,16},{28,20},{1,9},{5... | collective-permute-start | bytes 70664 | tf_op jit(solution)/shard_map/ppermute | solution.py:356
  15.4 2.2 %collective-permute-done.4 = f32[1,5888]{1,0:T(1,128)S(1)} collective-permute-done((f32[1,5888]{1,0:T(1,128)S(1)}, f32[1,5888]{1,0:T(1,128)S(1)}, u32[]{:S(2)}, u32[]{:S(2)}) %collective-permute-start.4) | collective-permute-done | bytes 23584 | tf_op jit(solution)/shard_map/ppermute | solution.py:356
  17.7 2.7 %collective-permute-start.5 = (f32[1,5888]{1,0:T(1,128)S(1)}, f32[1,5888]{1,0:T(1,128)S(1)}, u32[]{:S(2)}, u32[]{:S(2)}) collective-permute-start(f32[1,5888]{1,0:T(1,128)S(1)} %max.16), channel_id=1, source_target_pairs={{0,16},{4,20},{8,24},{12,28},{16,0},{20,4},{24,8},{28,12},{1,17},{... | collective-permute-start | bytes 70664 | tf_op jit(solution)/shard_map/ppermute | solution.py:356
  20.3 0.5 collective-permute-start.9
  20.8 0.5 collective-permute-start.14
  21.4 0.5 collective-permute-done.1.refs_2_
  21.9 0.6 collective-permute-done.5
  22.5 0.1 collective-permute-start.6
  22.6 2.0 %collective-permute-done.6.refs_1_ = f32[1,5888]{1,0:T(1,128)S(1)} collective-permute-done((f32[1,5888]{1,0:T(1,128)S(1)}, f32[1,5888]{1,0:T(1,128)S(1)}, u32[]{:S(2)}, u32[]{:S(2)}) %collective-permute-start.6) | collective-permute-done | bytes 23584 | tf_op jit(solution)/shard_map/ppermute | solution.py:356
  24.6 1.2 collective-permute-start.7
  25.8 12.9 %collective-permute-done.7.refs_2_ = f32[1,5888]{1,0:T(1,128)S(1)} collective-permute-done((f32[1,5888]{1,0:T(1,128)S(1)}, f32[1,5888]{1,0:T(1,128)S(1)}, u32[]{:S(2)}, u32[]{:S(2)}) %collective-permute-start.7) | collective-permute-done | bytes 23584 | tf_op jit(solution)/shard_map/ppermute | solution.py:356
  38.7 3.2 %collective-permute-done.8.refs_3_ = f32[1,5888]{1,0:T(1,128)S(1)} collective-permute-done((f32[1,5888]{1,0:T(1,128)S(1)}, f32[1,5888]{1,0:T(1,128)S(1)}, u32[]{:S(2)}, u32[]{:S(2)}) %collective-permute-start.8) | collective-permute-done | bytes 23584 | tf_op jit(solution)/shard_map/ppermute | solution.py:356
  41.9 0.7 collective-permute-start.10
  42.7 1.7 %scale_tables.1 = (f32[1792,8]{1,0:T(8,128)S(1)}, f32[8,1024]{1,0:T(8,128)S(1)}, f32[1,224]{1,0:T(1,128)}, f32[1,512]{1,0:T(1,128)}) custom-call(s32[2]{0:T(128)S(1)} %pad_add_fusion.where_ref, f32[1,5888]{1,0:T(1,128)S(1)} %maximum_maximum_fusion.refs_0_, f32[1,5888]{1,0:T(1,128)S(1)} %collective-permute-done.6.refs_1_, ...), custom_call_target="tpu_custom_call" | custom-call | tf_op jit(solution)/shard_map/scale_tables/pallas_call | solution.py:175
  44.4 1.4 %collective-permute-start.13 = (bf16[896,384]{1,0:T(8,128)(2,1)S(1)}, bf16[896,384]{1,0:T(8,128)(2,1)S(1)}, u32[]{:S(2)}, u32[]{:S(2)}) collective-permute-start(bf16[896,384]{1,0:T(8,128)(2,1)S(1)} %get-tuple-element.50.refs_2_), channel_id=1, source_target_pairs={{0,1},{1,0},{2,3},{3,2},{4,5},{5,4},{6,7},{7,6},{8,9},{9,8},{10,11... | collective-permute-start | bytes 2064392 | tf_op jit(solution)/shard_map/ppermute | solution.py:356
  45.8 3.7 %quantize_rows.1.refs_0_ = bf16[896,1536]{1,0:T(8,128)(2,1)S(1)} custom-call(bf16[896,384]{1,0:T(8,128)(2,1)S(1)} %get-tuple-element.39.refs_0_, bf16[896,384]{1,0:T(8,128)(2,1)S(1)} %collective-permute-done.refs_1_, bf16[896,384]{1,0:T(8,128)(2,1)S(1)} %collective-permute-done.1.refs_2_, bf16[896,384]{1,0:T(8,128)(2,1)S(1)} %collective-permute-done.2.refs_3_, ...), custom_call_target="tpu_custom_call" | custom-call | flops 2752512000 | bytes 5505024 | tf_op jit(solution)/shard_map/quantize_rows/pallas_call | solution.py:212
  49.6 2.2 %collective-permute-done.10.refs_4_ = bf16[384,384]{1,0:T(8,128)(2,1)S(1)} collective-permute-done((bf16[384,384]{1,0:T(8,128)(2,1)S(1)}, bf16[384,384]{1,0:T(8,128)(2,1)S(1)}, u32[]{:S(2)}, u32[]{:S(2)}) %collective-permute-start.10) | collective-permute-done | bytes 294944 | tf_op jit(solution)/shard_map/ppermute | solution.py:356
  51.8 0.7 collective-permute-start.18
  52.5 3.8 %collective-permute-done.11.refs_5_ = bf16[384,384]{1,0:T(8,128)(2,1)S(1)} collective-permute-done((bf16[384,384]{1,0:T(8,128)(2,1)S(1)}, bf16[384,384]{1,0:T(8,128)(2,1)S(1)}, u32[]{:S(2)}, u32[]{:S(2)}) %collective-permute-start.11) | collective-permute-done | bytes 294944 | tf_op jit(solution)/shard_map/ppermute | solution.py:356
  56.4 1.3 collective-permute-start.28
  57.7 1.6 %collective-permute-start.29 = (bf16[384,128]{1,0:T(8,128)(2,1)S(1)}, bf16[384,128]{1,0:T(8,128)(2,1)S(1)}, u32[]{:S(2)}, u32[]{:S(2)}) collective-permute-start(bf16[384,128]{1,0:T(8,128)(2,1)S(1)} %get-tuple-element.67), channel_id=1, source_target_pairs={{0,3},{1,2},{2,1},{3,0},{4,7},{5,6},{6,5},{7,4},{8,11},{9,10},{10,... | collective-permute-start | bytes 294920 | tf_op jit(solution)/shard_map/ppermute | solution.py:356
  59.3 3.2 %quantize_and_multiply.4 = (bf16[896,384]{1,0:T(8,128)(2,1)S(1)}, bf16[1536,384]{1,0:T(8,128)(2,1)S(1)}) custom-call(bf16[896,1536]{1,0:T(8,128)(2,1)S(1)} %quantize_rows.1.refs_0_, f32[8,1024]{1,0:T(8,128)S(1)} %get-tuple-element.43.refs_1_, bf16[384,1024]{1,0:T(8,128)(2,1)S(1)} %get-tuple-element.44.refs_2_, ...), custom_call_target="tpu_custom_call" | custom-call | flops 2113929216 | bytes 3932160 | tf_op jit(solution)/shard_map/quantize_and_multiply/pallas_call | solution.py:252
  62.5 0.2 collective-permute-done.28.refs_4_
  62.7 0.5 collective-permute-start.19
  63.2 1.5 %collective-permute-done.29.refs_5_ = bf16[384,128]{1,0:T(8,128)(2,1)S(1)} collective-permute-done((bf16[384,128]{1,0:T(8,128)(2,1)S(1)}, bf16[384,128]{1,0:T(8,128)(2,1)S(1)}, u32[]{:S(2)}, u32[]{:S(2)}) %collective-permute-start.29) | collective-permute-done | bytes 98336 | tf_op jit(solution)/shard_map/ppermute | solution.py:356
  64.7 0.9 collective-permute-start.23
  65.6 0.4 collective-permute-start.15
  66.0 1.5 %collective-permute-start.12 = (bf16[896,384]{1,0:T(8,128)(2,1)S(1)}, bf16[896,384]{1,0:T(8,128)(2,1)S(1)}, u32[]{:S(2)}, u32[]{:S(2)}) collective-permute-start(bf16[896,384]{1,0:T(8,128)(2,1)S(1)} %get-tuple-element.49), channel_id=1, source_target_pairs={{0,4},{4,0},{8,12},{12,8},{16,20},{20,16},{24,28},{28,24},{1,5},{5... | collective-permute-start | bytes 2064392 | tf_op jit(solution)/shard_map/ppermute | solution.py:356
  67.5 7.8 %input_gradient.1 = bf16[384,1792]{1,0:T(8,128)(2,1)} custom-call(bf16[384,4096]{1,0:T(8,128)(2,1)S(1)} %bitcast.6, bf16[1792,4096]{1,0:T(8,128)(2,1)S(1)} %copy-done.3), custom_call_target="tpu_custom_call" | custom-call | flops 5637144576 | bytes 17825792 | tf_op jit(solution)/shard_map/input_gradient/pallas_call | solution.py:123
  75.3 0.6 collective-permute-start.24
  76.0 2.0 %quantize_and_multiply.5 = (bf16[896,256]{1,0:T(8,128)(2,1)S(1)}, bf16[1536,256]{1,0:T(8,128)(2,1)S(1)}) custom-call(bf16[896,1536]{1,0:T(8,128)(2,1)S(1)} %quantize_rows.1.refs_0_, f32[8,1024]{1,0:T(8,128)S(1)} %get-tuple-element.43.refs_1_, bf16[384,1024]{1,0:T(8,128)(2,1)S(1)} %get-tuple-element.44.refs_2_, ...), custom_call_target="tpu_custom_call" | custom-call | flops 1409286144 | bytes 3538944 | tf_op jit(solution)/shard_map/quantize_and_multiply/pallas_call | solution.py:252
  78.0 0.6 collective-permute-start.20
  78.6 1.5 %quantize_and_multiply.7 = (bf16[896,128]{1,0:T(8,128)(2,1)S(1)}, bf16[1536,128]{1,0:T(8,128)(2,1)S(1)}) custom-call(bf16[896,1536]{1,0:T(8,128)(2,1)S(1)} %quantize_rows.1.refs_0_, f32[8,1024]{1,0:T(8,128)S(1)} %get-tuple-element.43.refs_1_, bf16[384,1024]{1,0:T(8,128)(2,1)S(1)} %get-tuple-element.44.refs_2_, ...), custom_call_target="tpu_custom_call" | custom-call | flops 704643072 | bytes 3145728 | tf_op jit(solution)/shard_map/quantize_and_multiply/pallas_call | solution.py:252
  80.1 2.4 %collective-permute-done.24.refs_5_ = bf16[384,256]{1,0:T(8,128)(2,1)S(1)} collective-permute-done((bf16[384,256]{1,0:T(8,128)(2,1)S(1)}, bf16[384,256]{1,0:T(8,128)(2,1)S(1)}, u32[]{:S(2)}, u32[]{:S(2)}) %collective-permute-start.24) | collective-permute-done | bytes 196640 | tf_op jit(solution)/shard_map/ppermute | solution.py:356
  82.5 0.5 collective-permute-start.30
  83.0 2.0 %quantize_and_multiply.6 = (bf16[896,256]{1,0:T(8,128)(2,1)S(1)}, bf16[1536,256]{1,0:T(8,128)(2,1)S(1)}) custom-call(bf16[896,1536]{1,0:T(8,128)(2,1)S(1)} %quantize_rows.1.refs_0_, f32[8,1024]{1,0:T(8,128)S(1)} %get-tuple-element.43.refs_1_, bf16[384,1024]{1,0:T(8,128)(2,1)S(1)} %get-tuple-element.44.refs_2_, ...), custom_call_target="tpu_custom_call" | custom-call | flops 1409286144 | bytes 3538944 | tf_op jit(solution)/shard_map/quantize_and_multiply/pallas_call | solution.py:252
  85.1 1.6 %collective-permute-start.25 = (bf16[896,256]{1,0:T(8,128)(2,1)S(1)}, bf16[896,256]{1,0:T(8,128)(2,1)S(1)}, u32[]{:S(2)}, u32[]{:S(2)}) collective-permute-start(bf16[896,256]{1,0:T(8,128)(2,1)S(1)} %get-tuple-element.63), channel_id=1, source_target_pairs={{0,4},{4,0},{8,12},{12,8},{16,20},{20,16},{24,28},{28,24},{1,5},{5... | collective-permute-start | bytes 1376264 | tf_op jit(solution)/shard_map/ppermute | solution.py:356
  86.7 5.4 %finish.4 = (bf16[448,384]{1,0:T(8,128)(2,1)S(1)}, f32[448,384]{1,0:T(8,128)S(1)}, bf16[896,1536]{1,0:T(8,128)(2,1)S(1)}) custom-call(bf16[1536,384]{1,0:T(8,128)(2,1)S(1)} %get-tuple-element.48.refs_0_, bf16[896,384]{1,0:T(8,128)(2,1)S(1)} %collective-permute-done.12.refs_1_, bf16[896,384]{1,0:T(8,128)(2,1)S(1)} %get-tuple-element.50.refs_2_, ...), custom_call_target="tpu_custom_call" | custom-call | flops 2113929216 | bytes 3932160 | tf_op jit(solution)/shard_map/finish/pallas_call | solution.py:319
  92.1 1.6 %collective-permute-start.16 = (bf16[448,384]{1,0:T(8,128)(2,1)S(1)}, bf16[448,384]{1,0:T(8,128)(2,1)S(1)}, u32[]{:S(2)}, u32[]{:S(2)}) collective-permute-start(bf16[448,384]{1,0:T(8,128)(2,1)S(1)} %get-tuple-element.52), channel_id=1, source_target_pairs={{0,8},{4,12},{8,0},{12,4},{16,24},{20,28},{24,16},{28,20},{1,9},{5... | collective-permute-start | bytes 1032200 | tf_op jit(solution)/shard_map/ppermute | solution.py:356
  93.7 5.3 %collective-permute-done.30.refs_1_ = bf16[896,128]{1,0:T(8,128)(2,1)S(1)} collective-permute-done((bf16[896,128]{1,0:T(8,128)(2,1)S(1)}, bf16[896,128]{1,0:T(8,128)(2,1)S(1)}, u32[]{:S(2)}, u32[]{:S(2)}) %collective-permute-start.30) | collective-permute-done | bytes 229408 | tf_op jit(solution)/shard_map/ppermute | solution.py:356
  99.0 1.4 %finish.7 = (bf16[448,128]{1,0:T(8,128)(2,1)S(1)}, f32[448,128]{1,0:T(8,128)S(1)}) custom-call(bf16[1536,128]{1,0:T(8,128)(2,1)S(1)} %get-tuple-element.68.refs_0_, bf16[896,128]{1,0:T(8,128)(2,1)S(1)} %collective-permute-done.30.refs_1_, bf16[896,1536]{1,0:T(8,128)(2,1)S(1)} %get-tuple-element.57.refs_2_), custom_call_target="tpu_custom_call" | custom-call | flops 704643072 | bytes 3145728 | tf_op jit(solution)/shard_map/finish/pallas_call | solution.py:319
  100.4 1.6 %collective-permute-start.31 = (bf16[448,128]{1,0:T(8,128)(2,1)S(1)}, bf16[448,128]{1,0:T(8,128)(2,1)S(1)}, u32[]{:S(2)}, u32[]{:S(2)}) collective-permute-start(bf16[448,128]{1,0:T(8,128)(2,1)S(1)} %get-tuple-element.71), channel_id=1, source_target_pairs={{0,8},{4,12},{8,0},{12,4},{16,24},{20,28},{24,16},{28,20},{1,9},{5... | collective-permute-start | bytes 344072 | tf_op jit(solution)/shard_map/ppermute | solution.py:356
  102.1 1.5 %finish.5 = (bf16[448,256]{1,0:T(8,128)(2,1)S(1)}, f32[448,256]{1,0:T(8,128)S(1)}) custom-call(bf16[1536,256]{1,0:T(8,128)(2,1)S(1)} %get-tuple-element.55.refs_0_, bf16[896,256]{1,0:T(8,128)(2,1)S(1)} %collective-permute-done.20.refs_1_, bf16[896,1536]{1,0:T(8,128)(2,1)S(1)} %get-tuple-element.57.refs_2_), custom_call_target="tpu_custom_call" | custom-call | flops 1409286144 | bytes 3538944 | tf_op jit(solution)/shard_map/finish/pallas_call | solution.py:319
  103.5 0.5 collective-permute-start.21
  104.0 2.2 %collective-permute-done.31 = bf16[448,128]{1,0:T(8,128)(2,1)S(1)} collective-permute-done((bf16[448,128]{1,0:T(8,128)(2,1)S(1)}, bf16[448,128]{1,0:T(8,128)(2,1)S(1)}, u32[]{:S(2)}, u32[]{:S(2)}) %collective-permute-start.31) | collective-permute-done | bytes 114720 | tf_op jit(solution)/shard_map/ppermute | solution.py:356
  106.3 1.7 %collective-permute-start.32 = (bf16[224,128]{1,0:T(8,128)(2,1)S(1)}, bf16[224,128]{1,0:T(8,128)(2,1)S(1)}, u32[]{:S(2)}, u32[]{:S(2)}) collective-permute-start(bf16[224,128]{1,0:T(8,128)(2,1)S(1)} %slice.55), channel_id=1, source_target_pairs={{0,16},{4,20},{8,24},{12,28},{16,0},{20,4},{24,8},{28,12},{1,17},{... | collective-permute-start | bytes 172040 | tf_op jit(solution)/shard_map/ppermute | solution.py:356
  108.0 1.5 %finish.6 = (bf16[448,256]{1,0:T(8,128)(2,1)S(1)}, f32[448,256]{1,0:T(8,128)S(1)}) custom-call(bf16[1536,256]{1,0:T(8,128)(2,1)S(1)} %get-tuple-element.62.refs_0_, bf16[896,256]{1,0:T(8,128)(2,1)S(1)} %collective-permute-done.25.refs_1_, bf16[896,1536]{1,0:T(8,128)(2,1)S(1)} %get-tuple-element.57.refs_2_), custom_call_target="tpu_custom_call" | custom-call | flops 1409286144 | bytes 3538944 | tf_op jit(solution)/shard_map/finish/pallas_call | solution.py:319
  109.5 2.0 %collective-permute-start.26 = (bf16[448,256]{1,0:T(8,128)(2,1)S(1)}, bf16[448,256]{1,0:T(8,128)(2,1)S(1)}, u32[]{:S(2)}, u32[]{:S(2)}) collective-permute-start(bf16[448,256]{1,0:T(8,128)(2,1)S(1)} %get-tuple-element.65), channel_id=1, source_target_pairs={{0,8},{4,12},{8,0},{12,4},{16,24},{20,28},{24,16},{28,20},{1,9},{5... | collective-permute-start | bytes 688136 | tf_op jit(solution)/shard_map/ppermute | solution.py:356
  111.6 1.6 %collective-permute-start.22 = (bf16[224,256]{1,0:T(8,128)(2,1)S(1)}, bf16[224,256]{1,0:T(8,128)(2,1)S(1)}, u32[]{:S(2)}, u32[]{:S(2)}) collective-permute-start(bf16[224,256]{1,0:T(8,128)(2,1)S(1)} %slice.54), channel_id=1, source_target_pairs={{0,16},{4,20},{8,24},{12,28},{16,0},{20,4},{24,8},{28,12},{1,17},{... | collective-permute-start | bytes 344072 | tf_op jit(solution)/shard_map/ppermute | solution.py:356
  113.2 5.5 %collective-permute-done.26 = bf16[448,256]{1,0:T(8,128)(2,1)S(1)} collective-permute-done((bf16[448,256]{1,0:T(8,128)(2,1)S(1)}, bf16[448,256]{1,0:T(8,128)(2,1)S(1)}, u32[]{:S(2)}, u32[]{:S(2)}) %collective-permute-start.26) | collective-permute-done | bytes 229408 | tf_op jit(solution)/shard_map/ppermute | solution.py:356
  118.9 1.3 collective-permute-start.27
  120.2 0.1 convert_add_fusion
  120.3 1.7 %collective-permute-start.17 = (bf16[224,384]{1,0:T(8,128)(2,1)S(1)}, bf16[224,384]{1,0:T(8,128)(2,1)S(1)}, u32[]{:S(2)}, u32[]{:S(2)}) collective-permute-start(bf16[224,384]{1,0:T(8,128)(2,1)S(1)} %slice.52), channel_id=1, source_target_pairs={{0,16},{4,20},{8,24},{12,28},{16,0},{20,4},{24,8},{28,12},{1,17},{... | collective-permute-start | bytes 516104 | tf_op jit(solution)/shard_map/ppermute | solution.py:356
  122.0 8.6 %collective-permute-done.27 = bf16[224,256]{1,0:T(8,128)(2,1)S(1)} collective-permute-done((bf16[224,256]{1,0:T(8,128)(2,1)S(1)}, bf16[224,256]{1,0:T(8,128)(2,1)S(1)}, u32[]{:S(2)}, u32[]{:S(2)}) %collective-permute-start.27) | collective-permute-done | bytes 114720 | tf_op jit(solution)/shard_map/ppermute | solution.py:356
  130.6 1.8 %collective-permute-done.17 = bf16[224,384]{1,0:T(8,128)(2,1)S(1)} collective-permute-done((bf16[224,384]{1,0:T(8,128)(2,1)S(1)}, bf16[224,384]{1,0:T(8,128)(2,1)S(1)}, u32[]{:S(2)}, u32[]{:S(2)}) %collective-permute-start.17) | collective-permute-done | bytes 172064 | tf_op jit(solution)/shard_map/ppermute | solution.py:356
  132.5 1.0 maximum_multiply_fusion
  (42 shorter events, 0.4 us)
Async XLA Ops:
  0.7 1.3 %copy-start.2 = (bf16[1,384,1792]{2,1,0:T(8,128)(2,1)S(1)}, bf16[1,384,1792]{2,1,0:T(8,128)(2,1)}, u32[]{:S(2)}) copy-start(bf16[1,384,1792]{2,1,0:T(8,128)(2,1)} %param.4) | copy-start | bytes 4128772
  3.4 18.5 %collective-permute-start.1 = (bf16[896,384]{1,0:T(8,128)(2,1)S(1)}, bf16[896,384]{1,0:T(8,128)(2,1)S(1)}, u32[]{:S(2)}, u32[]{:S(2)}) collective-permute-start(bf16[896,384]{1,0:T(8,128)(2,1)S(1)} %get-tuple-element.39.refs_0_), channel_id=1, source_target_pairs={{0,2},{1,3},{2,0},{3,1},{4,6},{5,7},{6,4},{7,5},{8,10},{9,11},{10,... | collective-permute-start | bytes 2064392 | tf_op jit(solution)/shard_map/ppermute | solution.py:356
  6.4 1.9 %copy-start = (bf16[1,384,4096]{2,1,0:T(8,128)(2,1)S(1)}, bf16[1,384,4096]{2,1,0:T(8,128)(2,1)}, u32[]{:S(2)}) copy-start(bf16[1,384,4096]{2,1,0:T(8,128)(2,1)} %param.3) | copy-start | bytes 9437188
  9.8 3.9 %collective-permute-start.3 = (f32[1,5888]{1,0:T(1,128)S(1)}, f32[1,5888]{1,0:T(1,128)S(1)}, u32[]{:S(2)}, u32[]{:S(2)}) collective-permute-start(f32[1,5888]{1,0:T(1,128)S(1)} %constant_dynamic-update-slice_fusion), channel_id=1, source_target_pairs={{0,4},{4,0},{8,12},{12,8},{16,20},{20,16},{24,28},{28,24},{1,5},{5... | collective-permute-start | bytes 70664 | tf_op jit(solution)/shard_map/ppermute | solution.py:356
  13.8 3.9 %collective-permute-start.4 = (f32[1,5888]{1,0:T(1,128)S(1)}, f32[1,5888]{1,0:T(1,128)S(1)}, u32[]{:S(2)}, u32[]{:S(2)}) collective-permute-start(f32[1,5888]{1,0:T(1,128)S(1)} %max.15), channel_id=1, source_target_pairs={{0,8},{4,12},{8,0},{12,4},{16,24},{20,28},{24,16},{28,20},{1,9},{5... | collective-permute-start | bytes 70664 | tf_op jit(solution)/shard_map/ppermute | solution.py:356
  17.7 4.8 %collective-permute-start.5 = (f32[1,5888]{1,0:T(1,128)S(1)}, f32[1,5888]{1,0:T(1,128)S(1)}, u32[]{:S(2)}, u32[]{:S(2)}) collective-permute-start(f32[1,5888]{1,0:T(1,128)S(1)} %max.16), channel_id=1, source_target_pairs={{0,16},{4,20},{8,24},{12,28},{16,0},{20,4},{24,8},{28,12},{1,17},{... | collective-permute-start | bytes 70664 | tf_op jit(solution)/shard_map/ppermute | solution.py:356
  20.3 22.3 %collective-permute-start = (bf16[896,384]{1,0:T(8,128)(2,1)S(1)}, bf16[896,384]{1,0:T(8,128)(2,1)S(1)}, u32[]{:S(2)}, u32[]{:S(2)}) collective-permute-start(bf16[896,384]{1,0:T(8,128)(2,1)S(1)} %get-tuple-element.39.refs_0_), channel_id=1, source_target_pairs={{0,1},{1,0},{2,3},{3,2},{4,5},{5,4},{6,7},{7,6},{8,9},{9,8},{10,11... | collective-permute-start | bytes 2064392 | tf_op jit(solution)/shard_map/ppermute | solution.py:356
  20.3 37.3 %collective-permute-start.9 = (bf16[384,1024]{1,0:T(8,128)(2,1)S(1)}, bf16[384,1024]{1,0:T(8,128)(2,1)S(1)}, u32[]{:S(2)}, u32[]{:S(2)}) collective-permute-start(bf16[384,1024]{1,0:T(8,128)(2,1)S(1)} %get-tuple-element.45), channel_id=1, source_target_pairs={{0,1},{1,0},{2,3},{3,2},{4,5},{5,4},{6,7},{7,6},{8,9},{9,8},{10,11... | collective-permute-start | bytes 2359304 | tf_op jit(solution)/shard_map/ppermute | solution.py:356
  20.8 44.8 %collective-permute-start.14 = (bf16[896,384]{1,0:T(8,128)(2,1)S(1)}, bf16[896,384]{1,0:T(8,128)(2,1)S(1)}, u32[]{:S(2)}, u32[]{:S(2)}) collective-permute-start(bf16[896,384]{1,0:T(8,128)(2,1)S(1)} %get-tuple-element.50.refs_2_), channel_id=1, source_target_pairs={{0,2},{1,3},{2,0},{3,1},{4,6},{5,7},{6,4},{7,5},{8,10},{9,11},{10,... | collective-permute-start | bytes 2064392 | tf_op jit(solution)/shard_map/ppermute | solution.py:356
  21.8 22.6 %collective-permute-start.2 = (bf16[896,384]{1,0:T(8,128)(2,1)S(1)}, bf16[896,384]{1,0:T(8,128)(2,1)S(1)}, u32[]{:S(2)}, u32[]{:S(2)}) collective-permute-start(bf16[896,384]{1,0:T(8,128)(2,1)S(1)} %collective-permute-done.1.refs_2_), channel_id=1, source_target_pairs={{0,1},{1,0},{2,3},{3,2},{4,5},{5,4},{6,7},{7,6},{8,9},{9,8},{10,11... | collective-permute-start | bytes 2064392 | tf_op jit(solution)/shard_map/ppermute | solution.py:356
  22.5 2.1 %collective-permute-start.6 = (f32[1,5888]{1,0:T(1,128)S(1)}, f32[1,5888]{1,0:T(1,128)S(1)}, u32[]{:S(2)}, u32[]{:S(2)}) collective-permute-start(f32[1,5888]{1,0:T(1,128)S(1)} %maximum_maximum_fusion.refs_0_), channel_id=1, source_target_pairs={{0,1},{1,0},{2,3},{3,2},{4,5},{5,4},{6,7},{7,6},{8,9},{9,8},{10,11... | collective-permute-start | bytes 70664 | tf_op jit(solution)/shard_map/ppermute | solution.py:356
  24.6 14.1 %collective-permute-start.7 = (f32[1,5888]{1,0:T(1,128)S(1)}, f32[1,5888]{1,0:T(1,128)S(1)}, u32[]{:S(2)}, u32[]{:S(2)}) collective-permute-start(f32[1,5888]{1,0:T(1,128)S(1)} %maximum_maximum_fusion.refs_0_), channel_id=1, source_target_pairs={{0,2},{1,3},{2,0},{3,1},{4,6},{5,7},{6,4},{7,5},{8,10},{9,11},{10,... | collective-permute-start | bytes 70664 | tf_op jit(solution)/shard_map/ppermute | solution.py:356
  38.7 3.2 %collective-permute-start.8 = (f32[1,5888]{1,0:T(1,128)S(1)}, f32[1,5888]{1,0:T(1,128)S(1)}, u32[]{:S(2)}, u32[]{:S(2)}) collective-permute-start(f32[1,5888]{1,0:T(1,128)S(1)} %maximum_maximum_fusion.refs_0_), channel_id=1, source_target_pairs={{0,3},{1,2},{2,1},{3,0},{4,7},{5,6},{6,5},{7,4},{8,11},{9,10},{10,... | collective-permute-start | bytes 70664 | tf_op jit(solution)/shard_map/ppermute | solution.py:356
  41.9 9.9 %collective-permute-start.10 = (bf16[384,384]{1,0:T(8,128)(2,1)S(1)}, bf16[384,384]{1,0:T(8,128)(2,1)S(1)}, u32[]{:S(2)}, u32[]{:S(2)}) collective-permute-start(bf16[384,384]{1,0:T(8,128)(2,1)S(1)} %get-tuple-element.46), channel_id=1, source_target_pairs={{0,2},{1,3},{2,0},{3,1},{4,6},{5,7},{6,4},{7,5},{8,10},{9,11},{10,... | collective-permute-start | bytes 884744 | tf_op jit(solution)/shard_map/ppermute | solution.py:356
  42.7 13.7 %collective-permute-start.11 = (bf16[384,384]{1,0:T(8,128)(2,1)S(1)}, bf16[384,384]{1,0:T(8,128)(2,1)S(1)}, u32[]{:S(2)}, u32[]{:S(2)}) collective-permute-start(bf16[384,384]{1,0:T(8,128)(2,1)S(1)} %get-tuple-element.47), channel_id=1, source_target_pairs={{0,3},{1,2},{2,1},{3,0},{4,7},{5,6},{6,5},{7,4},{8,11},{9,10},{10,... | collective-permute-start | bytes 884744 | tf_op jit(solution)/shard_map/ppermute | solution.py:356
  44.4 40.7 %collective-permute-start.13 = (bf16[896,384]{1,0:T(8,128)(2,1)S(1)}, bf16[896,384]{1,0:T(8,128)(2,1)S(1)}, u32[]{:S(2)}, u32[]{:S(2)}) collective-permute-start(bf16[896,384]{1,0:T(8,128)(2,1)S(1)} %get-tuple-element.50.refs_2_), channel_id=1, source_target_pairs={{0,1},{1,0},{2,3},{3,2},{4,5},{5,4},{6,7},{7,6},{8,9},{9,8},{10,11... | collective-permute-start | bytes 2064392 | tf_op jit(solution)/shard_map/ppermute | solution.py:356
  45.8 21.7 %copy-start.3 = (bf16[1792,4096]{1,0:T(8,128)(2,1)S(1)}, bf16[1792,4096]{1,0:T(8,128)(2,1)}, u32[]{:S(2)}) copy-start(bf16[1792,4096]{1,0:T(8,128)(2,1)} %right.1) | copy-start | bytes 44040196
  51.8 14.2 %collective-permute-start.18 = (bf16[384,256]{1,0:T(8,128)(2,1)S(1)}, bf16[384,256]{1,0:T(8,128)(2,1)S(1)}, u32[]{:S(2)}, u32[]{:S(2)}) collective-permute-start(bf16[384,256]{1,0:T(8,128)(2,1)S(1)} %get-tuple-element.53), channel_id=1, source_target_pairs={{0,2},{1,3},{2,0},{3,1},{4,6},{5,7},{6,4},{7,5},{8,10},{9,11},{10,... | collective-permute-start | bytes 589832 | tf_op jit(solution)/shard_map/ppermute | solution.py:356
  56.4 6.3 %collective-permute-start.28 = (bf16[384,128]{1,0:T(8,128)(2,1)S(1)}, bf16[384,128]{1,0:T(8,128)(2,1)S(1)}, u32[]{:S(2)}, u32[]{:S(2)}) collective-permute-start(bf16[384,128]{1,0:T(8,128)(2,1)S(1)} %get-tuple-element.66), channel_id=1, source_target_pairs={{0,2},{1,3},{2,0},{3,1},{4,6},{5,7},{6,4},{7,5},{8,10},{9,11},{10,... | collective-permute-start | bytes 294920 | tf_op jit(solution)/shard_map/ppermute | solution.py:356
  57.7 7.1 %collective-permute-start.29 = (bf16[384,128]{1,0:T(8,128)(2,1)S(1)}, bf16[384,128]{1,0:T(8,128)(2,1)S(1)}, u32[]{:S(2)}, u32[]{:S(2)}) collective-permute-start(bf16[384,128]{1,0:T(8,128)(2,1)S(1)} %get-tuple-element.67), channel_id=1, source_target_pairs={{0,3},{1,2},{2,1},{3,0},{4,7},{5,6},{6,5},{7,4},{8,11},{9,10},{10,... | collective-permute-start | bytes 294920 | tf_op jit(solution)/shard_map/ppermute | solution.py:356
  59.3 8.2 %copy-start.1 = (bf16[1,384,4096]{2,1,0:T(8,128)(2,1)S(1)}, bf16[1,384,4096]{2,1,0:T(8,128)(2,1)}, u32[]{:S(2)}) copy-start(bf16[1,384,4096]{2,1,0:T(8,128)(2,1)} %param.3) | copy-start | bytes 9437188
  62.7 12.6 %collective-permute-start.19 = (bf16[384,256]{1,0:T(8,128)(2,1)S(1)}, bf16[384,256]{1,0:T(8,128)(2,1)S(1)}, u32[]{:S(2)}, u32[]{:S(2)}) collective-permute-start(bf16[384,256]{1,0:T(8,128)(2,1)S(1)} %get-tuple-element.54), channel_id=1, source_target_pairs={{0,3},{1,2},{2,1},{3,0},{4,7},{5,6},{6,5},{7,4},{8,11},{9,10},{10,... | collective-permute-start | bytes 589832 | tf_op jit(solution)/shard_map/ppermute | solution.py:356
  64.7 13.2 %collective-permute-start.23 = (bf16[384,256]{1,0:T(8,128)(2,1)S(1)}, bf16[384,256]{1,0:T(8,128)(2,1)S(1)}, u32[]{:S(2)}, u32[]{:S(2)}) collective-permute-start(bf16[384,256]{1,0:T(8,128)(2,1)S(1)} %get-tuple-element.60), channel_id=1, source_target_pairs={{0,2},{1,3},{2,0},{3,1},{4,6},{5,7},{6,4},{7,5},{8,10},{9,11},{10,... | collective-permute-start | bytes 589832 | tf_op jit(solution)/shard_map/ppermute | solution.py:356
  65.6 21.1 %collective-permute-start.15 = (bf16[896,384]{1,0:T(8,128)(2,1)S(1)}, bf16[896,384]{1,0:T(8,128)(2,1)S(1)}, u32[]{:S(2)}, u32[]{:S(2)}) collective-permute-start(bf16[896,384]{1,0:T(8,128)(2,1)S(1)} %collective-permute-done.14.refs_4_), channel_id=1, source_target_pairs={{0,1},{1,0},{2,3},{3,2},{4,5},{5,4},{6,7},{7,6},{8,9},{9,8},{10,11... | collective-permute-start | bytes 2064392 | tf_op jit(solution)/shard_map/ppermute | solution.py:356
  66.0 20.7 %collective-permute-start.12 = (bf16[896,384]{1,0:T(8,128)(2,1)S(1)}, bf16[896,384]{1,0:T(8,128)(2,1)S(1)}, u32[]{:S(2)}, u32[]{:S(2)}) collective-permute-start(bf16[896,384]{1,0:T(8,128)(2,1)S(1)} %get-tuple-element.49), channel_id=1, source_target_pairs={{0,4},{4,0},{8,12},{12,8},{16,20},{20,16},{24,28},{28,24},{1,5},{5... | collective-permute-start | bytes 2064392 | tf_op jit(solution)/shard_map/ppermute | solution.py:356
  75.3 7.2 %collective-permute-start.24 = (bf16[384,256]{1,0:T(8,128)(2,1)S(1)}, bf16[384,256]{1,0:T(8,128)(2,1)S(1)}, u32[]{:S(2)}, u32[]{:S(2)}) collective-permute-start(bf16[384,256]{1,0:T(8,128)(2,1)S(1)} %get-tuple-element.61), channel_id=1, source_target_pairs={{0,3},{1,2},{2,1},{3,0},{4,7},{5,6},{6,5},{7,4},{8,11},{9,10},{10,... | collective-permute-start | bytes 589832 | tf_op jit(solution)/shard_map/ppermute | solution.py:356
  78.0 24.1 %collective-permute-start.20 = (bf16[896,256]{1,0:T(8,128)(2,1)S(1)}, bf16[896,256]{1,0:T(8,128)(2,1)S(1)}, u32[]{:S(2)}, u32[]{:S(2)}) collective-permute-start(bf16[896,256]{1,0:T(8,128)(2,1)S(1)} %get-tuple-element.56), channel_id=1, source_target_pairs={{0,4},{4,0},{8,12},{12,8},{16,20},{20,16},{24,28},{28,24},{1,5},{5... | collective-permute-start | bytes 1376264 | tf_op jit(solution)/shard_map/ppermute | solution.py:356
  82.5 16.5 %collective-permute-start.30 = (bf16[896,128]{1,0:T(8,128)(2,1)S(1)}, bf16[896,128]{1,0:T(8,128)(2,1)S(1)}, u32[]{:S(2)}, u32[]{:S(2)}) collective-permute-start(bf16[896,128]{1,0:T(8,128)(2,1)S(1)} %get-tuple-element.69), channel_id=1, source_target_pairs={{0,4},{4,0},{8,12},{12,8},{16,20},{20,16},{24,28},{28,24},{1,5},{5... | collective-permute-start | bytes 688136 | tf_op jit(solution)/shard_map/ppermute | solution.py:356
  85.1 22.9 %collective-permute-start.25 = (bf16[896,256]{1,0:T(8,128)(2,1)S(1)}, bf16[896,256]{1,0:T(8,128)(2,1)S(1)}, u32[]{:S(2)}, u32[]{:S(2)}) collective-permute-start(bf16[896,256]{1,0:T(8,128)(2,1)S(1)} %get-tuple-element.63), channel_id=1, source_target_pairs={{0,4},{4,0},{8,12},{12,8},{16,20},{20,16},{24,28},{28,24},{1,5},{5... | collective-permute-start | bytes 1376264 | tf_op jit(solution)/shard_map/ppermute | solution.py:356
  92.1 28.1 %collective-permute-start.16 = (bf16[448,384]{1,0:T(8,128)(2,1)S(1)}, bf16[448,384]{1,0:T(8,128)(2,1)S(1)}, u32[]{:S(2)}, u32[]{:S(2)}) collective-permute-start(bf16[448,384]{1,0:T(8,128)(2,1)S(1)} %get-tuple-element.52), channel_id=1, source_target_pairs={{0,8},{4,12},{8,0},{12,4},{16,24},{20,28},{24,16},{28,20},{1,9},{5... | collective-permute-start | bytes 1032200 | tf_op jit(solution)/shard_map/ppermute | solution.py:356
  100.4 5.8 %collective-permute-start.31 = (bf16[448,128]{1,0:T(8,128)(2,1)S(1)}, bf16[448,128]{1,0:T(8,128)(2,1)S(1)}, u32[]{:S(2)}, u32[]{:S(2)}) collective-permute-start(bf16[448,128]{1,0:T(8,128)(2,1)S(1)} %get-tuple-element.71), channel_id=1, source_target_pairs={{0,8},{4,12},{8,0},{12,4},{16,24},{20,28},{24,16},{28,20},{1,9},{5... | collective-permute-start | bytes 344072 | tf_op jit(solution)/shard_map/ppermute | solution.py:356
  103.5 8.0 %collective-permute-start.21 = (bf16[448,256]{1,0:T(8,128)(2,1)S(1)}, bf16[448,256]{1,0:T(8,128)(2,1)S(1)}, u32[]{:S(2)}, u32[]{:S(2)}) collective-permute-start(bf16[448,256]{1,0:T(8,128)(2,1)S(1)} %get-tuple-element.59), channel_id=1, source_target_pairs={{0,8},{4,12},{8,0},{12,4},{16,24},{20,28},{24,16},{28,20},{1,9},{5... | collective-permute-start | bytes 688136 | tf_op jit(solution)/shard_map/ppermute | solution.py:356
  106.3 5.2 %collective-permute-start.32 = (bf16[224,128]{1,0:T(8,128)(2,1)S(1)}, bf16[224,128]{1,0:T(8,128)(2,1)S(1)}, u32[]{:S(2)}, u32[]{:S(2)}) collective-permute-start(bf16[224,128]{1,0:T(8,128)(2,1)S(1)} %slice.55), channel_id=1, source_target_pairs={{0,16},{4,20},{8,24},{12,28},{16,0},{20,4},{24,8},{28,12},{1,17},{... | collective-permute-start | bytes 172040 | tf_op jit(solution)/shard_map/ppermute | solution.py:356
  109.5 9.3 %collective-permute-start.26 = (bf16[448,256]{1,0:T(8,128)(2,1)S(1)}, bf16[448,256]{1,0:T(8,128)(2,1)S(1)}, u32[]{:S(2)}, u32[]{:S(2)}) collective-permute-start(bf16[448,256]{1,0:T(8,128)(2,1)S(1)} %get-tuple-element.65), channel_id=1, source_target_pairs={{0,8},{4,12},{8,0},{12,4},{16,24},{20,28},{24,16},{28,20},{1,9},{5... | collective-permute-start | bytes 688136 | tf_op jit(solution)/shard_map/ppermute | solution.py:356
  111.6 10.4 %collective-permute-start.22 = (bf16[224,256]{1,0:T(8,128)(2,1)S(1)}, bf16[224,256]{1,0:T(8,128)(2,1)S(1)}, u32[]{:S(2)}, u32[]{:S(2)}) collective-permute-start(bf16[224,256]{1,0:T(8,128)(2,1)S(1)} %slice.54), channel_id=1, source_target_pairs={{0,16},{4,20},{8,24},{12,28},{16,0},{20,4},{24,8},{28,12},{1,17},{... | collective-permute-start | bytes 344072 | tf_op jit(solution)/shard_map/ppermute | solution.py:356
  118.9 11.7 %collective-permute-start.27 = (bf16[224,256]{1,0:T(8,128)(2,1)S(1)}, bf16[224,256]{1,0:T(8,128)(2,1)S(1)}, u32[]{:S(2)}, u32[]{:S(2)}) collective-permute-start(bf16[224,256]{1,0:T(8,128)(2,1)S(1)} %slice.53), channel_id=1, source_target_pairs={{0,16},{4,20},{8,24},{12,28},{16,0},{20,4},{24,8},{28,12},{1,17},{... | collective-permute-start | bytes 344072 | tf_op jit(solution)/shard_map/ppermute | solution.py:356
  120.3 12.2 %collective-permute-start.17 = (bf16[224,384]{1,0:T(8,128)(2,1)S(1)}, bf16[224,384]{1,0:T(8,128)(2,1)S(1)}, u32[]{:S(2)}, u32[]{:S(2)}) collective-permute-start(bf16[224,384]{1,0:T(8,128)(2,1)S(1)} %slice.52), channel_id=1, source_target_pairs={{0,16},{4,20},{8,24},{12,28},{16,0},{20,4},{24,8},{28,12},{1,17},{... | collective-permute-start | bytes 516104 | tf_op jit(solution)/shard_map/ppermute | solution.py:356
